TPU v7x, 256 devices: a whole 4x4x8 slice. The times are simulated.
256 devices in a mesh: lat: 16 (over y, x_lo, core), lon: 16 (over z, x_hi).
Axes of the slice: x: 4 (x_hi: 2, x_lo: 2; x = x_hi * 2 + x_lo), y: 4, z: 8, core: 2. Of those that a mesh axis runs over, the one named last changes fastest.
Arguments:
- adjoint: float32 [8, 8, 512, 2048], P(None, None, 'lat', 'lon'), may hold values from -6 to 6
- transport: float32 [6, 8, 512, 2048], P(None, None, 'lat', 'lon'), may hold values from 0.03 to 0.14
- cell_weight: float32 [512, 2048], P('lat', 'lon'), may hold values from 0.1 to 1
- region_local: int32 [512, 2048], P('lat', 'lon'), may hold values from 0 to 255
- tile_regions: int32 [256, 256], replicated, may hold values from 0 to 16383, as said below
- polar_rows: int32 [512], P('lat'), may hold values 0 or 1
- week_index: int32 [1], replicated, may hold values from 0 to 51
- grad_in: bfloat16 [16384, 416], P(('lat', 'lon')), may hold values from -6 to 6
- covariance: bfloat16 [16384, 16384], P(('lat', 'lon')), may hold values from -0.1875 to 0.1875
Outputs:
- adjoint_out: float32 [8, 8, 512, 2048], P(None, None, 'lat', 'lon')
- precond: float32 [16384, 416], P(('lat', 'lon'))
Inputs may be any that keep to these rules, and one draw needn't show every extreme that they name: `tile_regions`: each row holds 256 different region numbers; with per = 1, entries o * per to o * per + per - 1 of a row lie in regions o * 64 to o * 64 + 63, for every o.
All inputs are finite; a program needn't handle non-finite values. No bound on the sum of `polar_rows` on one device may be relied on, other than what follows from the above.
Results may differ from a plain program's by a relative error of at most 0.00066.
Values may be sent and summed in bfloat16 or wider, within the bound.
A program may use at most 128 MiB of HBM per device.

v0:
```python
import functools

import jax
import jax.numpy as jnp
from jax import lax
from jax.sharding import Mesh
from jax.sharding import PartitionSpec as P

LON = ("lon_0", "lon_1")
LAT_LON = ("lat", "lon_0", "lon_1")


def extended_2(x, sides, width):
    for axis, dim in sides:
        size, length = (lax.axis_size(axis), x.shape[dim])
        up = [(i, (i + 1) % size) for i in range(size)]
        down = [(j, i) for i, j in up]
        last = lax.slice_in_dim(x, length - width, length, axis=dim)
        leading = lax.slice_in_dim(x, 0, width, axis=dim)
        before = lax.ppermute(last, axis, up)
        after = lax.ppermute(leading, axis, down)
        x = jnp.concatenate([before, x, after], axis=dim)
    return x


def one_axis_at_a_time(x, axes):
    return functools.reduce(lax.psum, axes, x)


def advance(padded, rates):
    centre = padded[:, :, 1:-1, 1:-1]
    to_east = padded[:, :, 1:-1, 2:] - centre
    to_west = padded[:, :, 1:-1, :-2] - centre
    to_north = padded[:, :, 2:, 1:-1] - centre
    to_south = padded[:, :, :-2, 1:-1] - centre
    flat_zero = jnp.zeros_like(centre[:, :1])
    upper = jnp.concatenate([centre[:, 1:] - centre[:, :-1], flat_zero], axis=1)
    lower = jnp.concatenate([flat_zero, centre[:, :-1] - centre[:, 1:]], axis=1)
    return (
        centre
        + rates[0] * to_east
        + rates[1] * to_west
        + rates[2] * to_north
        + rates[3] * to_south
        + rates[4] * upper
        + rates[5] * lower
    )


def pole_mask(padded, margin, interior):
    band = lax.axis_index("lat")
    last_band = lax.axis_size("lat") - 1
    row_ids = jnp.arange(interior + 2 * margin, dtype=jnp.int32)
    outside = (row_ids < margin) & (band == 0) | (row_ids >= interior + margin) & (
        band == last_band
    )
    return jnp.where(outside[None, None, :, None], 0.0, padded)


def shards(
    adjoint,
    transport,
    cell_weight,
    region_local,
    tile_regions,
    polar_rows,
    week_index,
    grad_in,
    covariance,
):
    tracers, levels, lat_rows, lon_cols = adjoint.shape
    region_count = covariance.shape[1]
    own_rows = covariance.shape[0]
    week_cols = grad_in.shape[1] // tracers
    lon_count = lax.axis_size(LON)
    my_tile = lax.axis_index("lat") * lon_count + lax.axis_index(LON)
    base = jnp.dot(
        covariance,
        lax.all_gather(grad_in, LAT_LON, axis=0, tiled=True),
        preferred_element_type=jnp.float32,
    )
    extended, rate_ext = (
        extended_2(adjoint, (("lat", 2), (LON, 3)), 2),
        extended_2(transport, (("lat", 2), (LON, 3)), 2),
    )
    extended = pole_mask(extended, 2, lat_rows)
    first = advance(extended, rate_ext[:, :, 1:-1, 1:-1])
    first = pole_mask(first, 1, lat_rows)
    field = advance(first, transport)
    row_sums = one_axis_at_a_time(jnp.sum(field, axis=3), LON)
    zonal = row_sums / (lon_cols * lon_count)
    flags = polar_rows.astype(jnp.float32)[None, None, :, None]
    adjoint_out = field + 0.5 * flags * (zonal[..., None] - field)
    surface = (adjoint_out[:, 0] * cell_weight[None]).reshape(tracers, -1)
    local_count = tile_regions.shape[1]
    one_hot = (
        region_local.reshape(1, -1) == jnp.arange(local_count, dtype=jnp.int32)[:, None]
    ).astype(jnp.float32)
    local_sums = lax.dot_general(
        one_hot,
        surface,
        (((1,), (1,)), ((), ())),
        precision=lax.Precision.HIGHEST,
        preferred_element_type=jnp.float32,
    )
    my_regions = lax.dynamic_index_in_dim(tile_regions, my_tile, 0, keepdims=False)
    dense = jnp.zeros((region_count, tracers), jnp.float32).at[my_regions].add(local_sums)
    fresh_all = lax.psum(dense, LAT_LON).astype(jnp.bfloat16)
    added = jnp.dot(covariance, fresh_all, preferred_element_type=jnp.float32)
    week_hot = (jnp.arange(week_cols, dtype=jnp.int32) == week_index[0]).astype(jnp.float32)
    precond = (
        base.reshape(own_rows, week_cols, tracers) + week_hot[None, :, None] * added[:, None, :]
    )
    return (adjoint_out, precond.reshape(own_rows, week_cols * tracers))


def solution(mesh):
    split = Mesh(mesh.devices.reshape(mesh.shape["lat"], 8, 2), ("lat", "lon_0", "lon_1"))
    placed = (
        P(None, None, "lat", LON),
        P(None, None, "lat", LON),
        P("lat", LON),
        P("lat", LON),
        P(),
        P("lat"),
        P(),
        P(LAT_LON, None),
        P(LAT_LON, None),
    )
    return jax.shard_map(
        shards,
        mesh=split,
        in_specs=placed,
        out_specs=(P(None, None, "lat", LON), P(LAT_LON, None)),
        check_vma=False,
    )
```

profile of v0, /device:TPU:1, one launch (start us, length us, event | category | flops | bytes accessed | tf_op | source)
XLA Modules:
  0.0 763.2 jit_solution(8474163198109357353)
XLA Ops:
  9.0 2.7 collective-permute-start.4
  15.8 2.7 collective-permute-start.1
  22.3 3.1 copy.74
  26.1 2.2 copy.73
  33.4 5.3 collective-permute-start.7
  38.7 2.6 copy.69
  50.3 4.4 maximum_bitcast_fusion.4
  54.7 3.5 copy.68
  58.2 3.4 copy.70
  63.0 5.1 collective-permute-start.3
  68.1 3.1 maximum_bitcast_fusion.3
  71.2 2.5 maximum_select_fusion
  73.8 4.2 slice_subtract_fusion.9
  78.0 6.3 fusion.4
  86.7 6.9 fusion.33
  93.6 20.9 %psum.21 = f32[8,8,32]{2,1,0:T(8,128)S(1)} all-reduce(f32[8,8,32]{2,1,0:T(8,128)S(1)} %get-tuple-element.10), channel_id=1, replica_groups=mesh['lat'=16,'lon_0'=8,'lon_1'=2] {'lon_0'}, use_global_device_ids=true, to_apply=%region_1.2 | all-reduce | flops 2048 | bytes 16384 | tf_op jit(solution)/shard_map/psum | solution.py:27
  114.5 10.1 %psum.22 = f32[8,8,32]{2,1,0:T(8,128)S(1)} all-reduce(f32[8,8,32]{2,1,0:T(8,128)S(1)} %psum.21), channel_id=1, replica_groups=mesh['lat'=16,'lon_0'=8,'lon_1'=2] {'lon_1'}, use_global_device_ids=true, to_apply=%region_2.3 | all-reduce | flops 2048 | bytes 16384 | tf_op jit(solution)/shard_map/psum | solution.py:27
  124.6 2.7 multiply_add_fusion
  129.2 3.8 copy.85
  135.3 5.2 scatter_custom_fusion
  140.5 153.3 %all-reduce.5 = bf16[16384,8]{1,0:T(8,128)(2,1)} all-reduce(f32[16384,8]{1,0:T(8,128)} %scatter_custom_fusion), channel_id=1, replica_groups=mesh['lat'=16,'lon_0'=8,'lon_1'=2] {'lat','lon_0','lon_1'}, use_global_device_ids=true, to_apply=%region_4.5 | all-reduce | flops 131072 | bytes 786432 | tf_op jit(solution)/shard_map/psum | solution.py:108
  293.7 3.4 fusion.27
  297.3 449.6 %all-gather.2.cloned.1.call-done = bf16[16384,416]{1,0:T(8,128)(2,1)} async-done(((bf16[64,416]{1,0:T(8,128)(2,1)}), bf16[16384,416]{1,0:T(8,128)(2,1)}) %all-gather.2.cloned.1.call-update) | async-done | bytes 13631504 | tf_op jit(solution)/shard_map/all_gather | solution.py:79
  746.9 9.4 %convolution_add_fusion = f32[64,416]{1,0:T(8,128)} fusion(bf16[64,16384]{1,0:T(8,128)(2,1)S(1)} %copy-done, bf16[16384,416]{1,0:T(8,128)(2,1)} %all-gather.2.cloned.1.call-done, f32[64,416]{1,0:T(8,128)S(1)} %copy.84, f32[416]{0:T(512)S(1)} %mul.213), kind=kOutput, calls=%fused_computation.43 | convolution fusion | flops 872468480 | bytes 15943296 | tf_op jit(solution)/shard_map/dot_general | solution.py:77
  (81 shorter events, 31.6 us)
Async XLA Ops:
  7.2 286.6 %copy-start = (bf16[64,16384]{1,0:T(8,128)(2,1)S(1)}, bf16[64,16384]{1,0:T(8,128)(2,1)}, u32[]{:S(2)}) copy-start(bf16[64,16384]{1,0:T(8,128)(2,1)} %param.17) | copy-start | bytes 6291460
  7.2 739.8 %all-gather.2.cloned.1.call-start = ((), (), s32[]{:S(2)}) async-start(), calls=%async_computation | async-start | bytes 16842752 | tf_op jit(solution)/shard_map/all_gather | solution.py:79
  9.0 17.1 %collective-permute-start.4 = (f32[6,8,2,128]{3,1,2,0:T(8,128)S(1)}, f32[6,8,2,128]{3,1,2,0:T(8,128)S(1)}, u32[]{:S(2)}, u32[]{:S(2)}) collective-permute-start(f32[6,8,2,128]{3,1,2,0:T(8,128)S(1)} %copy.89), channel_id=1, source_target_pairs={{0,16},{16,32},{32,48},{48,64},{64,80},{80,96},{96,112},{112,128},... | collective-permute-start | bytes 147464 | tf_op jit(solution)/shard_map/ppermute | solution.py:20
  11.7 16.7 %collective-permute-start.5 = (f32[6,8,2,128]{3,1,2,0:T(8,128)S(1)}, f32[6,8,2,128]{3,1,2,0:T(8,128)S(1)}, u32[]{:S(2)}, u32[]{:S(2)}) collective-permute-start(f32[6,8,2,128]{3,1,2,0:T(8,128)S(1)} %copy.90), channel_id=1, source_target_pairs={{16,0},{32,16},{48,32},{64,48},{80,64},{96,80},{112,96},{128,112},... | collective-permute-start | bytes 147464 | tf_op jit(solution)/shard_map/ppermute | solution.py:21
  14.1 40.6 %collective-permute-start = (f32[8,8,2,128]{3,1,2,0:T(8,128)}, f32[8,8,2,128]{3,1,2,0:T(8,128)}, u32[]{:S(2)}, u32[]{:S(2)}) collective-permute-start(f32[8,8,2,128]{3,1,2,0:T(8,128)} %copy.87), channel_id=1, source_target_pairs={{0,16},{16,32},{32,48},{48,64},{64,80},{80,96},{96,112},{112,128},... | collective-permute-start | bytes 196616 | tf_op jit(solution)/shard_map/ppermute | solution.py:20
  15.8 42.4 %collective-permute-start.1 = (f32[8,8,2,128]{3,1,2,0:T(8,128)}, f32[8,8,2,128]{3,1,2,0:T(8,128)}, u32[]{:S(2)}, u32[]{:S(2)}) collective-permute-start(f32[8,8,2,128]{3,1,2,0:T(8,128)} %copy.88), channel_id=1, source_target_pairs={{16,0},{32,16},{48,32},{64,48},{80,64},{96,80},{112,96},{128,112},... | collective-permute-start | bytes 196616 | tf_op jit(solution)/shard_map/ppermute | solution.py:21
  30.6 8.1 %copy-start.14 = (f32[8,8,32,128]{3,2,1,0:T(8,128)S(1)}, f32[8,8,32,128]{3,2,1,0:T(8,128)}, u32[]{:S(2)}) copy-start(f32[8,8,32,128]{3,2,1,0:T(8,128)} %param.9) | copy-start | bytes 3145732
  32.3 17.9 %collective-permute-start.6 = (f32[6,8,36,2]{2,1,3,0:T(8,128)}, f32[6,8,36,2]{2,1,3,0:T(8,128)}, u32[]{:S(2)}, u32[]{:S(2)}) collective-permute-start(f32[6,8,36,2]{2,1,3,0:T(8,128)} %get-tuple-element.20), channel_id=1, source_target_pairs={{0,1},{1,2},{2,3},{3,4},{4,5},{5,6},{6,7},{7,8},{8,9},{9,10},{10,1... | collective-permute-start | bytes 41480 | tf_op jit(solution)/shard_map/ppermute | solution.py:20
  33.4 16.9 %collective-permute-start.7 = (f32[6,8,36,2]{2,1,3,0:T(8,128)}, f32[6,8,36,2]{2,1,3,0:T(8,128)}, u32[]{:S(2)}, u32[]{:S(2)}) collective-permute-start(f32[6,8,36,2]{2,1,3,0:T(8,128)} %get-tuple-element.21), channel_id=1, source_target_pairs={{1,0},{2,1},{3,2},{4,3},{5,4},{6,5},{7,6},{8,7},{9,8},{10,9},{11,1... | collective-permute-start | bytes 41480 | tf_op jit(solution)/shard_map/ppermute | solution.py:21
  61.6 6.5 copy-start.1
  61.6 6.5 copy-start.2
  61.6 6.5 copy-start.3
  61.6 9.6 %copy-start.6 = (f32[8,8,2,128]{2,1,3,0:T(8,128)S(1)}, f32[8,8,2,128]{2,1,3,0:T(8,128)}, u32[]{:S(2)}) copy-start(f32[8,8,2,128]{2,1,3,0:T(8,128)} %copy.70) | copy-start | bytes 196612
  62.9 8.3 %collective-permute-start.2 = (f32[8,8,36,2]{2,1,3,0:T(8,128)S(1)}, f32[8,8,36,2]{2,1,3,0:T(8,128)S(1)}, u32[]{:S(2)}, u32[]{:S(2)}) collective-permute-start(f32[8,8,36,2]{2,1,3,0:T(8,128)S(1)} %get-tuple-element.12), channel_id=1, source_target_pairs={{0,1},{1,2},{2,3},{3,4},{4,5},{5,6},{6,7},{7,8},{8,9},{9,10},{10,1... | collective-permute-start | bytes 55304 | tf_op jit(solution)/shard_map/ppermute | solution.py:20
  63.0 8.2 %copy-start.4 = (f32[8,8,32,128]{2,1,3,0:T(8,128)S(1)}, f32[8,8,32,128]{2,1,3,0:T(8,128)}, u32[]{:S(2)}) copy-start(f32[8,8,32,128]{2,1,3,0:T(8,128)} %copy.69) | copy-start | bytes 3145732
  63.0 8.2 %copy-start.5 = (f32[8,8,2,128]{2,1,3,0:T(8,128)S(1)}, f32[8,8,2,128]{2,1,3,0:T(8,128)}, u32[]{:S(2)}) copy-start(f32[8,8,2,128]{2,1,3,0:T(8,128)} %copy.68) | copy-start | bytes 196612
  63.0 8.2 %collective-permute-start.3 = (f32[8,8,36,2]{2,1,3,0:T(8,128)S(1)}, f32[8,8,36,2]{2,1,3,0:T(8,128)S(1)}, u32[]{:S(2)}, u32[]{:S(2)}) collective-permute-start(f32[8,8,36,2]{2,1,3,0:T(8,128)S(1)} %get-tuple-element.13), channel_id=1, source_target_pairs={{1,0},{2,1},{3,2},{4,3},{5,4},{6,5},{7,6},{8,7},{9,8},{10,9},{11,1... | collective-permute-start | bytes 55304 | tf_op jit(solution)/shard_map/ppermute | solution.py:21
  73.8 4.3 copy-start.8
  73.8 4.2 copy-start.15
  84.4 2.3 copy-start.9
  84.4 2.3 copy-start.10
  129.2 4.1 copy-start.16
  129.2 4.1 copy-start.17
  129.2 3.8 slice-start
  (4 other events, 8.8 us)
Sparse Core Ops, SparseCore 0:
  9.9 737.0 all-gather.1
where the time goes:
time: 767 us; the launch traced here: 763 us
  waiting for transfers between devices  450 us (59%)
  blocking collectives  184 us (24%)
  other arithmetic  42.6 us (6%)
  local copies, waits for them, and re-layouts  37.6 us (5%)
  starting transfers between devices  18.7 us (2%)
  between operations  15 us (2%)
  matrix products  14.8 us (2%)
    all_gather x1, waiting for transfers between devices, shards(): lax.all_gather(grad_in, LAT_LON, axis=0, tiled=True)  450 us
    psum x1, blocking collectives, shards(): fresh_all = lax.psum(dense, LAT_LON).astype(jnp.bfloat16)  153 us
    psum x2, blocking collectives, one_axis_at_a_time(): return functools.reduce(lax.psum, axes, x)  30.9 us
  transfers between devices with their start and end apart: 9, of which 1 were waited for; matrix products, arithmetic and copies ran while one was open for 11% of the time, Pallas kernels for 0%

commit v1 on v0

v1 whole, which is shorter than its diff:
```python
import functools

import jax
import jax.numpy as jnp
from jax import lax
from jax.experimental import pallas as pl
from jax.experimental.pallas import tpu as pltpu
from jax.sharding import PartitionSpec as P

MESH = pl.DeviceIdType.MESH
F32 = jnp.float32
BF16 = jnp.bfloat16
ALL = slice(None)


def dot(a, b):
    return lax.dot_general(a, b, (((1,), (0,)), ((), ())), preferred_element_type=F32)


def dot_nt(a, b):
    return lax.dot_general(a, b, (((1,), (1,)), ((), ())), preferred_element_type=F32)


def kernel(
    adj, tr, weight, rl, flag, reg, grad, week, cov,
    aout, pre,
    first, surf, b0, b1, b2, cmat, fr, col_s, row_n, row_s, col_e, col_w, halo_n, halo_s,
    zbuf, mbuf, xbuf, ybuf, obuf, pacc, precv, aacc, arecv,
    ssem, rsem, lsem,
):
    lat = lax.axis_index("lat")
    lon = lax.axis_index("lon")
    core = lax.rem(lat, 2)
    xl = lax.rem(lat // 2, 2)
    y = lat // 4
    z = lon // 2
    xh = lax.rem(lon, 2)
    x = xh * 2 + xl
    me = {"x": x, "y": y, "z": z}
    size = {"x": 4, "y": 4, "z": 8}
    counter = [0]
    sends = []

    def wrap(v, n):
        return lax.rem(v + 2 * n, n)

    def device(c, at_core):
        return ((c["y"] * 2 + lax.rem(c["x"], 2)) * 2 + at_core, c["z"] * 2 + c["x"] // 2)

    def remote(src, dst, to, k):
        return pltpu.make_async_remote_copy(
            src_ref=src, dst_ref=dst, send_sem=ssem.at[k], recv_sem=rsem.at[k],
            device_id=to, device_id_type=MESH,
        )

    def send(src, dst, to, k):
        c = remote(src, dst, to, k)
        c.start()
        sends.append(c)

    def take(count=1):
        k = counter[0]
        counter[0] += count
        return k

    def arrived(dst, k):
        remote(dst, dst, (lat, lon), k).wait_recv()

    other = (lat + 1 - 2 * core, lon)

    barrier = pltpu.get_barrier_semaphore()
    for k in range(1, 16):
        pl.semaphore_signal(barrier, inc=1, device_id=(lat, wrap(lon + k, 16)), device_id_type=MESH)
        pl.semaphore_signal(barrier, inc=1, device_id=(wrap(lat + k, 16), lon), device_id_type=MESH)
    pl.semaphore_signal(
        barrier, inc=1, device_id=(lat + 2 - 4 * xl, lon + 1 - 2 * xh), device_id_type=MESH
    )

    own_cov = []
    for g in range(8):
        c = pltpu.make_async_copy(
            cov.at[:, pl.ds(pl.multiple_of((g * 2 + core) * 1024, 1024), 1024)],
            cmat.at[g, pl.ds(pl.multiple_of(core * 64, 64), 64), :],
            lsem.at[g],
        )
        c.start()
        own_cov.append(c)

    lane = lax.broadcasted_iota(jnp.int32, (32, 128), 1)
    row = lax.broadcasted_iota(jnp.int32, (32, 128), 0)

    b0[y, xl, z, xh, 0:64, :] = grad[:, 0:128]
    b1[y, xl, z, xh] = grad[:, 128:256]
    b2[y, xl, z, xh] = grad[:, 256:384]
    tail = jnp.zeros((16, 128), F32)
    for q in range(4):
        sel = (
            lax.broadcasted_iota(jnp.int32, (32, 128), 1)
            == lax.broadcasted_iota(jnp.int32, (32, 128), 0) + 32 * q
        ).astype(F32).astype(BF16)
        tail = tail + dot(grad[16 * q:16 * q + 16, 384:416], sel)
    b0[y, xl, z, xh, 64:80, :] = tail.astype(BF16)

    def edges(step, j, v, acc):
        row_n[step, pl.ds(j, 1), :] = v[31:32, :]
        row_s[step, pl.ds(j, 1), :] = v[0:1, :]
        acc = jnp.where(lane == j, pltpu.roll(v, lax.rem(j + 1, 128), 1), acc)
        return jnp.where(lane == j + 64, pltpu.roll(v, j + 64, 1), acc)

    def pack(j, acc):
        return edges(0, j, adj[j], acc)

    col_s[0] = lax.fori_loop(0, 64, pack, jnp.zeros((32, 128), F32), unroll=4)

    pl.semaphore_wait(barrier, 31)

    east, west = wrap(lon + 1, 16), wrap(lon - 1, 16)
    north, south = wrap(lat + 1, 16), wrap(lat - 1, 16)

    def halo_send(s):
        k = take(4)
        send(col_s.at[s], col_w.at[s], (lat, east), k)
        send(col_s.at[s], col_e.at[s], (lat, west), k + 1)
        send(row_n.at[s], halo_s.at[s], (north, lon), k + 2)
        send(row_s.at[s], halo_n.at[s], (south, lon), k + 3)
        return k

    def halo_wait(s, k):
        arrived(col_w.at[s], k)
        arrived(col_e.at[s], k + 1)
        arrived(halo_s.at[s], k + 2)
        arrived(halo_n.at[s], k + 3)

    parts = {
        "a": (b0, "zyx", 48),
        "b": (b1, "yxz", 32),
        "c": (b2, "zxy", 32),
    }

    def slot(buf, at, rows):
        yi = at["y"] if at["y"] is not None else ALL
        zi = at["z"] if at["z"] is not None else ALL
        if at["x"] is None:
            return buf.at[yi, :, zi, :, rows]
        return buf.at[yi, lax.rem(at["x"], 2), zi, at["x"] // 2, rows]

    def whole(buf):
        return pl.ds(0, buf.shape[4])

    ids = {}

    def direct_start(p):
        buf, order, _ = parts[p]
        d = order[0]
        n = size[d]
        k = take(n - 1)
        ids[p, 1] = k
        for i in range(1, n):
            to = dict(me)
            to[d] = wrap(me[d] + i, n)
            here = slot(buf, me, whole(buf))
            send(here, here, device(to, core), k + i - 1)

    def direct_wait(p):
        buf, order, _ = parts[p]
        d = order[0]
        n = size[d]
        for i in range(1, n):
            at = dict(me)
            at[d] = wrap(me[d] - i, n)
            arrived(slot(buf, at, whole(buf)), ids[p, 1] + i - 1)

    def ring(p, stage, s):
        buf, order, half = parts[p]
        d = order[stage - 1]
        n = size[d]
        at = {c: (None if c in order[:stage - 1] else me[c]) for c in "xyz"}
        last = s == n // 2
        rows_r = pl.ds(0, half) if last else whole(buf)
        rows_l = pl.ds(half, buf.shape[4] - half) if last else whole(buf)
        return buf, d, n, at, rows_r, rows_l

    def ring_start(p, stage, s):
        buf, d, n, at, rows_r, rows_l = ring(p, stage, s)
        k = take(2)
        ids[p, stage, s] = k
        right, left = dict(me), dict(me)
        right[d] = wrap(me[d] + 1, n)
        left[d] = wrap(me[d] - 1, n)
        fwd, back = dict(at), dict(at)
        fwd[d] = wrap(me[d] - (s - 1), n)
        back[d] = wrap(me[d] + (s - 1), n)
        src = slot(buf, fwd, rows_r)
        send(src, src, device(right, core), k)
        src = slot(buf, back, rows_l)
        send(src, src, device(left, core), k + 1)

    def ring_wait(p, stage, s):
        buf, d, n, at, rows_r, rows_l = ring(p, stage, s)
        k = ids[p, stage, s]
        fwd, back = dict(at), dict(at)
        fwd[d] = wrap(me[d] - s, n)
        back[d] = wrap(me[d] + s, n)
        arrived(slot(buf, fwd, rows_r), k)
        arrived(slot(buf, back, rows_l), k + 1)

    plan = {}
    for p, (_, order, _) in parts.items():
        steps = [(stage, s) for stage in (2, 3) for s in range(1, size[order[stage - 1]] // 2 + 1)]
        plan[p] = steps

    def pump(p, i):
        steps = plan[p]
        if i == 1:
            direct_wait(p)
        else:
            ring_wait(p, *steps[i - 2])
        if i <= len(steps):
            ring_start(p, *steps[i - 1])

    k1 = halo_send(0)
    for p in "bac":
        direct_start(p)
    k_cov = take(8)
    for g in range(8):
        send(
            cov.at[:, pl.ds(pl.multiple_of((g * 2 + 1 - core) * 1024, 1024), 1024)],
            cmat.at[g, pl.ds(pl.multiple_of(core * 64, 64), 64), :],
            other, k_cov + g,
        )

    has_north = (lat < 15).astype(F32)
    has_south = (lat > 0).astype(F32)

    def stencil(src, step, j):
        l = lax.rem(j, 8)
        c = src[j]
        ce = col_e[step]
        cw = col_w[step]
        e = pltpu.roll(jnp.where(lane == 0, pltpu.roll(ce, 64 - j, 1), c), 127, 1)
        v = pltpu.roll(jnp.where(lane == 127, pltpu.roll(cw, 127 - j, 1), c), 1, 1)
        n = jnp.where(row == 31, has_north * halo_n[step, pl.ds(j, 1), :], pltpu.roll(c, 31, 0))
        s = jnp.where(row == 0, has_south * halo_s[step, pl.ds(j, 1), :], pltpu.roll(c, 1, 0))
        u = src[j + jnp.minimum(7 - l, 1)]
        d = src[j - jnp.minimum(l, 1)]
        return (
            c + tr[l] * (e - c) + tr[8 + l] * (v - c) + tr[16 + l] * (n - c)
            + tr[24 + l] * (s - c) + tr[32 + l] * (u - c) + tr[40 + l] * (d - c)
        )

    halo_wait(0, k1)

    def step_one(j, acc):
        v = stencil(adj, 0, j)
        first[j] = v
        return edges(1, j, v, acc)

    col_s[1] = lax.fori_loop(0, 64, step_one, jnp.zeros((32, 128), F32), unroll=2)
    k2 = halo_send(1)
    pump("b", 1)
    pump("a", 1)
    pump("c", 1)
    halo_wait(1, k2)

    def step_two(j, acc):
        v = stencil(first, 1, j)
        aout[j] = v
        return jnp.where(lane == j, jnp.sum(v, axis=1, keepdims=True), acc)

    sums = lax.fori_loop(0, 64, step_two, jnp.zeros((32, 128), F32), unroll=2)
    lane16 = lax.broadcasted_iota(jnp.int32, (16, 128), 1)
    row16 = lax.broadcasted_iota(jnp.int32, (16, 128), 0)
    zbuf[lon] = jnp.where(lane16 < 64, sums[0:16], pltpu.roll(sums[16:32], 64, 1))
    kz = take(15)
    for i in range(1, 16):
        send(zbuf.at[lon], zbuf.at[lon], (lat, wrap(lon + i, 16)), kz + i - 1)
    pump("b", 2)
    pump("a", 2)
    pump("c", 2)
    pump("b", 3)
    for i in range(1, 16):
        arrived(zbuf.at[wrap(lon - i, 16)], kz + i - 1)
    total = zbuf[0]
    for i in range(1, 16):
        total = total + zbuf[i]
    total = total * (1.0 / 2048.0)
    mean = jnp.concatenate([total, pltpu.roll(total, 64, 1)], axis=0)
    flags = 0.5 * flag[...]

    def filtered(j):
        v = aout[j]
        return v + flags * (jnp.sum(jnp.where(lane == j, mean, 0.0), axis=1, keepdims=True) - v)

    for t in range(8):
        surf[t] = filtered(8 * t) * weight[...]

    pump("a", 3)
    pump("c", 3)

    sub8 = lax.broadcasted_iota(jnp.int32, (16, 128), 0)

    def regions(r, acc):
        lhs, rhs = [], [[], [], []]
        for h in range(2):
            i = 2 * r + h
            local = rl[pl.ds(i, 1), :]
            low = jnp.broadcast_to(local & 15, (16, 128))
            high = jnp.broadcast_to(local >> 4, (8, 128))
            lhs.append((low == sub8).astype(F32).astype(BF16))
            s = jnp.concatenate([surf[t, pl.ds(i, 1), :] for t in range(8)], axis=0)
            for n in range(3):
                piece = s.astype(BF16).astype(F32)
                s = s - piece
                rhs[n].append(
                    jnp.concatenate([jnp.where(high == a, piece, 0.0) for a in range(16)], axis=0).astype(BF16)
                )
        left = jnp.concatenate(lhs, axis=1)
        for n in range(3):
            acc = acc + dot_nt(left, jnp.concatenate(rhs[n], axis=1))
        return acc

    m = lax.fori_loop(0, 16, regions, jnp.zeros((16, 128), F32))
    for i in range(16):
        mbuf[i] = m[i:i + 1, :]
    xbuf[lon] = mbuf[lon]
    kx = take(15)
    for i in range(1, 16):
        to = wrap(lon + i, 16)
        send(mbuf.at[to], xbuf.at[lon], (lat, to), kx + i - 1)

    def rest(j, carry):
        aout[j] = filtered(j)
        return carry

    lax.fori_loop(0, 64, rest, 0, unroll=2)
    pump("b", 4)
    for i in range(1, 16):
        arrived(xbuf.at[wrap(lon - i, 16)], kx + i - 1)
    got = jnp.concatenate([xbuf[i] for i in range(16)], axis=0)
    turned = jnp.zeros((16, 128), F32)
    group = lane16 // 8
    for d in range(16):
        moved = got if d == 0 else pltpu.roll(pltpu.roll(got, 16 - d, 0), 8 * d, 1)
        turned = jnp.where(lax.rem(group - row16 + 16, 16) == d, moved, turned)
    for i in range(16):
        ybuf[i] = turned[i:i + 1, :]
    obuf[lat] = ybuf[lat]
    ky = take(15)
    for i in range(1, 16):
        to = wrap(lat + i, 16)
        send(ybuf.at[to], obuf.at[lat], (to, lon), ky + i - 1)
    pump("b", 5)
    for i in range(1, 16):
        arrived(obuf.at[wrap(lat - i, 16)], ky + i - 1)

    lane8 = lax.broadcasted_iota(jnp.int32, (8, 128), 1)
    row8 = lax.broadcasted_iota(jnp.int32, (8, 128), 0)
    packed = jnp.zeros((8, 128), F32)
    for v in range(8):
        f = jnp.zeros((8, 128), F32)
        for a in range(16):
            f = f + jnp.where(reg[a:a + 1, :] == row8 + 8 * v, obuf[a], 0.0)
        for shift in (64, 32, 16, 8):
            f = f + pltpu.roll(f, shift, 1)
        packed = jnp.where(lane8 // 8 == v, f, packed)
    fr[y, xl, z, xh] = packed.astype(BF16).astype(F32)
    kf = take(15)
    for i in range(1, 16):
        here = fr.at[y, xl, z, xh]
        send(here, here, (lat, wrap(lon + i, 16)), kf + i - 1)
    pump("a", 4)
    pump("c", 4)
    for i in range(1, 16):
        o = wrap(lon - i, 16)
        arrived(fr.at[y, xl, o // 2, lax.rem(o, 2)], kf + i - 1)
    kg = take(7)
    for i in range(1, 8):
        g = wrap(lat // 2 + i, 8)
        send(fr.at[y, xl], fr.at[y, xl], (g * 2 + core, lon), kg + i - 1)
    pump("b", 6)
    pump("a", 5)
    pump("c", 5)
    pump("b", 7)
    for c in own_cov:
        c.wait()
    for g in range(8):
        arrived(cmat.at[g, pl.ds(pl.multiple_of((1 - core) * 64, 64), 64), :], k_cov + g)

    pacc[...] = jnp.zeros((2, 64, 512), F32)

    def product(g, carry):
        gy, gx = g // 2, lax.rem(g, 2)
        c = cmat[g]
        r0 = jnp.concatenate(
            [b0[gy, gx][:, :, 0:64].reshape(1024, 128), b1[gy, gx].reshape(1024, 128)], axis=1
        )
        left = dot(c, r0)
        pacc[0, :, 0:256] += left[0:64]
        pacc[1, :, 0:256] += left[64:128]
        tails = b0[gy, gx][:, :, 64:80].reshape(256, 128)
        pieces = []
        for q in range(4):
            sel = (
                lax.broadcasted_iota(jnp.int32, (128, 128), 0)
                == lax.broadcasted_iota(jnp.int32, (128, 128), 1) + 32 * q
            ).astype(F32).astype(BF16)
            pieces.append(dot(tails, sel).astype(BF16).reshape(16, 16, 128))
        last = jnp.concatenate(pieces, axis=1).reshape(1024, 128)
        right = dot(c, jnp.concatenate([b2[gy, gx].reshape(1024, 128), last], axis=1))
        pacc[0, :, 256:512] += right[0:64]
        pacc[1, :, 256:512] += right[64:128]
        return carry

    lax.fori_loop(0, 8, product, 0)
    kp = take()
    send(pacc.at[1 - core], precv, other, kp)

    for i in range(1, 8):
        g = wrap(lat // 2 - i, 8)
        arrived(fr.at[g // 2, lax.rem(g, 2)], kg + i - 1)

    def fresh_product(g, acc):
        f = fr[g // 2, lax.rem(g, 2)].reshape(16, 8, 128)
        lanes = lax.broadcasted_iota(jnp.int32, (16, 8, 128), 2) // 8
        w = jnp.concatenate([jnp.where(lanes == v, f, 0.0) for v in range(8)], axis=1)
        return acc + dot(cmat[g], w.astype(BF16).reshape(1024, 128))

    added = lax.fori_loop(0, 8, fresh_product, jnp.zeros((128, 128), F32))
    for shift in (64, 32, 16, 8):
        added = added + pltpu.roll(added, shift, 1)
    aacc[0] = added[0:64]
    aacc[1] = added[64:128]
    ka = take()
    send(aacc.at[1 - core], arecv, other, ka)
    arrived(precv, kp)
    arrived(arecv, ka)
    mine = aacc[core] + arecv[...]
    base = pacc[core] + precv[...]
    for n in range(4):
        week_of = (lax.broadcasted_iota(jnp.int32, (64, 128), 1) + 128 * n) // 8
        pre[:, 128 * n:128 * n + 128] = base[:, 128 * n:128 * n + 128] + jnp.where(
            week_of == week[...], mine, 0.0
        )
    for c in sends:
        c.wait_send()


COPIES = 160


def shards(adjoint, transport, cell_weight, region_local, tile_regions, polar_rows, week_index, grad_in, covariance):
    me = lax.axis_index("lat") * 16 + lax.axis_index("lon")
    flag = jnp.broadcast_to(polar_rows.astype(F32)[:, None], (32, 128))
    owned = lax.dynamic_slice_in_dim(tile_regions, me, 1, axis=1).reshape(16, 16) - me * 64
    reg = jnp.broadcast_to(owned[:, :, None], (16, 16, 8)).reshape(16, 128)
    week = jnp.broadcast_to(week_index.reshape(1, 1), (64, 128))
    vmem = pl.BlockSpec(memory_space=pltpu.VMEM)
    aout, pre = pl.pallas_call(
        kernel,
        out_shape=(
            jax.ShapeDtypeStruct((64, 32, 128), F32),
            jax.ShapeDtypeStruct((64, 512), F32),
        ),
        in_specs=[vmem] * 8 + [pl.BlockSpec(memory_space=pl.ANY)],
        out_specs=(vmem, vmem),
        scratch_shapes=[
            pltpu.VMEM((64, 32, 128), F32),
            pltpu.VMEM((8, 32, 128), F32),
            pltpu.VMEM((4, 2, 8, 2, 80, 128), BF16),
            pltpu.VMEM((4, 2, 8, 2, 64, 128), BF16),
            pltpu.VMEM((4, 2, 8, 2, 64, 128), BF16),
            pltpu.VMEM((8, 128, 1024), BF16),
            pltpu.VMEM((4, 2, 8, 2, 8, 128), F32),
            pltpu.VMEM((2, 32, 128), F32),
            pltpu.VMEM((2, 64, 128), F32),
            pltpu.VMEM((2, 64, 128), F32),
            pltpu.VMEM((2, 32, 128), F32),
            pltpu.VMEM((2, 32, 128), F32),
            pltpu.VMEM((2, 64, 128), F32),
            pltpu.VMEM((2, 64, 128), F32),
            pltpu.VMEM((16, 16, 128), F32),
            pltpu.VMEM((16, 1, 128), F32),
            pltpu.VMEM((16, 1, 128), F32),
            pltpu.VMEM((16, 1, 128), F32),
            pltpu.VMEM((16, 1, 128), F32),
            pltpu.VMEM((2, 64, 512), F32),
            pltpu.VMEM((64, 512), F32),
            pltpu.VMEM((2, 64, 128), F32),
            pltpu.VMEM((64, 128), F32),
            pltpu.SemaphoreType.DMA((COPIES,)),
            pltpu.SemaphoreType.DMA((COPIES,)),
            pltpu.SemaphoreType.DMA((8,)),
        ],
        compiler_params=pltpu.CompilerParams(
            collective_id=0, has_side_effects=True, vmem_limit_bytes=40 * 1024 * 1024
        ),
        name="window",
    )(
        adjoint.reshape(64, 32, 128),
        transport.reshape(48, 32, 128),
        cell_weight, region_local, flag, reg, grad_in, week, covariance,
    )
    return aout.reshape(8, 8, 32, 128), pre[:, :416]


def solution(mesh):
    both = ("lat", "lon")
    return jax.shard_map(
        shards,
        mesh=mesh,
        in_specs=(
            P(None, None, "lat", "lon"), P(None, None, "lat", "lon"), P("lat", "lon"), P("lat", "lon"),
            P(), P("lat"), P(), P(both, None), P(both, None),
        ),
        out_specs=(P(None, None, "lat", "lon"), P(both, None)),
        check_vma=False,
    )
```

time: 767 us -> 96.5 us (0.13)
  waiting for transfers between devices: 450 us -> 0 us
  blocking collectives: 184 us -> 0 us
  Pallas kernels: 0 us -> 84.9 us
  other arithmetic: 42.6 us -> 1.75 us
  local copies, waits for them, and re-layouts: 37.6 us -> 8.15 us
  starting transfers between devices: 18.7 us -> 0 us
  matrix products: 14.8 us -> 0 us
  between operations: 15 us -> 1.31 us
    all_gather x1 -> x0, waiting for transfers between devices: 450 us -> none  [shards(): lax.all_gather(grad_in, LAT_LON, axis=0, tiled=True)]
    psum x3 -> x0, blocking collectives: 184 us -> none  [the longest x1 153 us: shards(): fresh_all = lax.psum(dense, LAT_LON).astype(jnp.bfloat16)]
    pallas_call x0 -> x1, Pallas kernels: none -> 84.9 us  [shards(): pl.pallas_call(kernel, out_shape=(jax.ShapeDtypeStruct((64, 32, 128), F32...]
    ppermute x8 -> x0, starting transfers between devices: 18.6 us -> none  [the longest x4 13.8 us: extended_2(): after = lax.ppermute(leading, axis, down)]
    dot_general x3 -> x0, matrix products: 14.8 us -> none  [the longest x1 9.42 us: shards(): jnp.dot(covariance, lax.all_gather(grad_in, LAT_LON, axis=0, tiled=True),...]
    ppermute x4 -> x0, local copies, waits for them, and re-layouts: 11.3 us -> none  [the longest x2 5.71 us: extended_2(): before = lax.ppermute(last, axis, up)]
    mul x11 -> x0, local copies, waits for them, and re-layouts: 11 us -> none  [the longest x2 3.85 us: advance(): rates[0] * to_east]
    select_n x3 -> x0, other arithmetic: 9.57 us -> none  [the longest x2 8.86 us: pole_mask(): return jnp.where(outside[None, None, :, None], 0.0, padded)]
  transfers between devices with their start and end apart: 9 -> 0, of which waited for: 1 -> 0; matrix products, arithmetic and copies ran while one was open for 11% -> 0% of each run, Pallas kernels for 0% -> 0%
where the time goes in v1:
time: 96.5 us; the launch traced here: 96.1 us
  Pallas kernels  84.9 us (88%)
  local copies, waits for them, and re-layouts  8.15 us (8%)
  other arithmetic  1.75 us (2%)
  between operations  1.31 us (1%)
    pallas_call x1, Pallas kernels, shards(): pl.pallas_call(kernel, out_shape=(jax.ShapeDtypeStruct((64, 32, 128), F32...  84.9 us
    unnamed x14, local copies, waits for them, and re-layouts  7.87 us

profile of v1, /device:TPU:1, one launch (start us, length us, event | category | flops | bytes accessed | tf_op | source)
XLA Modules:
  0.0 96.1 jit_solution(11527494769147560462)
XLA Ops:
  1.3 1.1 %subtract_reduce_fusion = s32[256]{0:T(256)S(1)} fusion(s32[256,256]{1,0:T(8,128)} %param.13, s32[]{:T(128)S(6)} %select_n.3, s32[]{:T(128)S(6)} %mul.7), kind=kLoop, calls=%fused_computation | loop fusion | flops 256 | bytes 2056 | tf_op jit(solution)/shard_map/sub | solution.py:454
  2.4 0.7 convert_element_type.3
  3.0 0.1 sub.15
  3.1 0.1 copy.11
  3.2 0.1 broadcast_in_dim.8.flag
  3.3 0.1 copy.12.reg
  3.3 0.0 copy-start
  3.3 1.6 %copy-done = bf16[64,16384]{1,0:T(8,128)(2,1)S(1)} copy-done((bf16[64,16384]{1,0:T(8,128)(2,1)S(1)}, bf16[64,16384]{1,0:T(8,128)(2,1)}, u32[]{:S(2)}) %copy-start) | copy-done | bytes 2097176
  4.9 0.0 copy-start.1
  4.9 1.2 %copy-done.1 = f32[8,8,32,128]{3,2,1,0:T(8,128)S(1)} copy-done((f32[8,8,32,128]{3,2,1,0:T(8,128)S(1)}, f32[8,8,32,128]{3,2,1,0:T(8,128)}, u32[]{:S(2)}) %copy-start.1) | copy-done | bytes 1048600
  6.2 0.0 copy-start.2
  6.2 1.1 %copy-done.2 = f32[6,8,32,128]{3,2,1,0:T(8,128)S(1)} copy-done((f32[6,8,32,128]{3,2,1,0:T(8,128)S(1)}, f32[6,8,32,128]{3,2,1,0:T(8,128)}, u32[]{:S(2)}) %copy-start.2) | copy-done | bytes 786456
  7.3 0.0 copy-start.3
  7.3 0.8 copy-done.3
  8.1 0.0 copy-start.4
  8.1 0.7 copy-done.4
  8.9 0.0 copy-start.5
  8.9 0.7 copy-done.5
  9.6 84.9 %window.1 = (f32[64,32,128]{2,1,0:T(8,128)S(1)}, f32[64,512]{1,0:T(8,128)S(1)}) custom-call(f32[64,32,128]{2,1,0:T(8,128)S(1)} %bitcast.9, f32[48,32,128]{2,1,0:T(8,128)S(1)} %bitcast.10, f32[32,128]{1,0:T(8,128)S(1)} %copy-done.4, s32[32,128]{1,0:T(8,128)S(1)} %copy-done.5, f32[32,128]{1,0:T(8,128)S(1)} %broadcast_in_dim.8.flag, s32[16,128]{1,0:T(8,128)S(1)} %copy.12.reg, ...), custom_call_target="tpu_custom_call" | custom-call | tf_op jit(solution)/shard_map/window/pallas_call | solution.py:458
  94.5 1.0 %copy.16 = f32[8,8,32,128]{3,2,1,0:T(8,128)} copy(f32[8,8,32,128]{3,2,1,0:T(8,128)S(1)} %bitcast.8) | data formatting | bytes 2097152
  95.5 0.7 copy.17
  (2 shorter events, 0.0 us)
Async XLA Ops:
  3.3 1.6 %copy-start = (bf16[64,16384]{1,0:T(8,128)(2,1)S(1)}, bf16[64,16384]{1,0:T(8,128)(2,1)}, u32[]{:S(2)}) copy-start(bf16[64,16384]{1,0:T(8,128)(2,1)} %cov.1) | copy-start | bytes 6291460
  4.9 1.2 %copy-start.1 = (f32[8,8,32,128]{3,2,1,0:T(8,128)S(1)}, f32[8,8,32,128]{3,2,1,0:T(8,128)}, u32[]{:S(2)}) copy-start(f32[8,8,32,128]{3,2,1,0:T(8,128)} %param.9) | copy-start | bytes 3145732
  6.2 1.1 %copy-start.2 = (f32[6,8,32,128]{3,2,1,0:T(8,128)S(1)}, f32[6,8,32,128]{3,2,1,0:T(8,128)}, u32[]{:S(2)}) copy-start(f32[6,8,32,128]{3,2,1,0:T(8,128)} %param.10) | copy-start | bytes 2359300
  7.3 0.8 copy-start.3
  8.1 0.7 copy-start.4
  8.9 0.7 copy-start.5

commit v2 on v1

v2 whole, which is shorter than its diff:
```python
import functools

import jax
import jax.numpy as jnp
from jax import lax
from jax.experimental import pallas as pl
from jax.experimental.pallas import tpu as pltpu
from jax.sharding import PartitionSpec as P

MESH = pl.DeviceIdType.MESH
F32 = jnp.float32
BF16 = jnp.bfloat16
ALL = slice(None)


def dot(a, b):
    return lax.dot_general(a, b, (((1,), (0,)), ((), ())), preferred_element_type=F32)


def dot_nt(a, b):
    return lax.dot_general(a, b, (((1,), (1,)), ((), ())), preferred_element_type=F32)


def kernel(
    adj_h, tr_h, weight_h, rl_h, tiles_h, polar_h, week_h, grad, cov,
    aout_h, pre_h,
    adj, tr, weight, rl, tiles, polar, week, gtail,
    first, surf, b0, b1, b2, cmat, fr, col_s, row_n, row_s, col_e, col_w, halo_n, halo_s,
    zbuf, ybar, mbuf, xbuf, ybuf, obuf, pacc, precv, aacc, arecv,
    aout, pre, ssem, rsem, lsem, insem,
):
    lat = lax.axis_index("lat")
    lon = lax.axis_index("lon")
    core = lax.rem(lat, 2)
    xl = lax.rem(lat // 2, 2)
    y = lat // 4
    z = lon // 2
    xh = lax.rem(lon, 2)
    x = xh * 2 + xl
    me = {"x": x, "y": y, "z": z}
    size = {"x": 4, "y": 4, "z": 8}
    counter = [0]
    sends = []

    def wrap(v, n):
        return lax.rem(v + 2 * n, n)

    def device(c, at_core):
        return ((c["y"] * 2 + lax.rem(c["x"], 2)) * 2 + at_core, c["z"] * 2 + c["x"] // 2)

    def remote(src, dst, to, k):
        return pltpu.make_async_remote_copy(
            src_ref=src, dst_ref=dst, send_sem=ssem.at[k], recv_sem=rsem.at[k],
            device_id=to, device_id_type=MESH,
        )

    def send(src, dst, to, k):
        c = remote(src, dst, to, k)
        c.start()
        sends.append(c)

    def take(count=1):
        k = counter[0]
        counter[0] += count
        return k

    def arrived(dst, k):
        remote(dst, dst, (lat, lon), k).wait_recv()

    other = (lat + 1 - 2 * core, lon)

    cur = [None]

    def mark(n):
        if PROFILE:
            if cur[0] is not None:
                cur[0].__exit__(None, None, None)
            cur[0] = jax.named_scope(n) if n else None
            if n:
                cur[0].__enter__()

    mark("s00_entry")
    barrier = pltpu.get_barrier_semaphore()
    for k in range(1, 16):
        pl.semaphore_signal(barrier, inc=1, device_id=(lat, wrap(lon + k, 16)), device_id_type=MESH)
        pl.semaphore_signal(barrier, inc=1, device_id=(wrap(lat + k, 16), lon), device_id_type=MESH)
    pl.semaphore_signal(
        barrier, inc=1, device_id=(lat + 2 - 4 * xl, lon + 1 - 2 * xh), device_id_type=MESH
    )

    def load(src, dst, k):
        c = pltpu.make_async_copy(src, dst, insem.at[k])
        c.start()
        return c

    in_adj = [load(adj_h.at[:, l], adj.at[l], l) for l in range(8)]
    in_grad = [
        load(grad.at[:, 0:128], b0.at[y, xl, z, xh, 0:64], 8),
        load(grad.at[:, 128:256], b1.at[y, xl, z, xh], 9),
        load(grad.at[:, 256:384], b2.at[y, xl, z, xh], 10),
        load(grad, gtail, 11),
    ]
    in_tr = load(tr_h, tr, 12)
    number = lat * 16 + lon
    lanes_at = pl.multiple_of(number // 128 * 128, 128)
    in_late = [
        load(weight_h, weight, 13), load(rl_h, rl, 14), load(polar_h, polar, 15),
        load(tiles_h.at[:, pl.ds(lanes_at, 128)], tiles, 16), load(week_h, week, 17),
    ]
    own_cov = []
    for g in range(8):
        c = pltpu.make_async_copy(
            cov.at[:, pl.ds(pl.multiple_of((g * 2 + core) * 1024, 1024), 1024)],
            cmat.at[g, pl.ds(pl.multiple_of(core * 64, 64), 64), :],
            lsem.at[g],
        )
        c.start()
        own_cov.append(c)

    lane = lax.broadcasted_iota(jnp.int32, (32, 128), 1)
    row = lax.broadcasted_iota(jnp.int32, (32, 128), 0)

    def edges(step, j, v, acc):
        row_n[step, pl.ds(j, 1), :] = v[31:32, :]
        row_s[step, pl.ds(j, 1), :] = v[0:1, :]
        return jnp.where(lane // 2 == j, pltpu.roll(v, lax.rem(2 * j + 1, 128), 1), acc)

    def pack(j, acc):
        return edges(0, j, adj[j // 8, lax.rem(j, 8)], acc)

    none = jnp.zeros((32, 128), F32)
    in_adj[0].wait()
    in_adj[1].wait()
    col_s[0] = lax.fori_loop(0, 16, pack, none, unroll=4)
    for c in in_adj[2:]:
        c.wait()
    col_s[1] = lax.fori_loop(16, 64, pack, none, unroll=4)

    for c in in_grad:
        c.wait()
    tail = jnp.zeros((16, 128), F32)
    for q in range(4):
        sel = (
            lax.broadcasted_iota(jnp.int32, (32, 128), 1)
            == lax.broadcasted_iota(jnp.int32, (32, 128), 0) + 32 * q
        ).astype(F32).astype(BF16)
        tail = tail + dot(gtail[16 * q:16 * q + 16, 384:416], sel)
    b0[y, xl, z, xh, 64:80, :] = tail.astype(BF16)

    mark("s01_barrier")
    pl.semaphore_wait(barrier, 31)
    mark("s02_send1")

    east, west = wrap(lon + 1, 16), wrap(lon - 1, 16)
    north, south = wrap(lat + 1, 16), wrap(lat - 1, 16)

    def halo_send(s, i, lo, hi):
        k = take(4)
        rows = pl.ds(lo, hi - lo)
        send(row_n.at[s, rows], halo_s.at[s, rows], (north, lon), k + 2)
        send(row_s.at[s, rows], halo_n.at[s, rows], (south, lon), k + 3)
        send(col_s.at[2 * s + i], col_w.at[2 * s + i], (lat, east), k)
        send(col_s.at[2 * s + i], col_e.at[2 * s + i], (lat, west), k + 1)
        return k

    def halo_wait(s, i, lo, hi, k):
        rows = pl.ds(lo, hi - lo)
        arrived(col_w.at[2 * s + i], k)
        arrived(col_e.at[2 * s + i], k + 1)
        arrived(halo_s.at[s, rows], k + 2)
        arrived(halo_n.at[s, rows], k + 3)
        return jnp.where(lax.rem(lane, 2) == 1, col_e[2 * s + i], pltpu.roll(col_w[2 * s + i], 2, 1))

    parts = {
        "a": (b0, "zyx", 48),
        "b": (b1, "yxz", 32),
        "c": (b2, "zxy", 32),
    }

    def slot(buf, at, rows):
        yi = at["y"] if at["y"] is not None else ALL
        zi = at["z"] if at["z"] is not None else ALL
        if at["x"] is None:
            return buf.at[yi, :, zi, :, rows]
        return buf.at[yi, lax.rem(at["x"], 2), zi, at["x"] // 2, rows]

    def whole(buf):
        return pl.ds(0, buf.shape[4])

    ids = {}

    def direct_start(p):
        buf, order, _ = parts[p]
        d = order[0]
        n = size[d]
        k = take(n - 1)
        ids[p, 1] = k
        for i in range(1, n):
            to = dict(me)
            to[d] = wrap(me[d] + i, n)
            here = slot(buf, me, whole(buf))
            send(here, here, device(to, core), k + i - 1)

    def direct_wait(p):
        buf, order, _ = parts[p]
        d = order[0]
        n = size[d]
        for i in range(1, n):
            at = dict(me)
            at[d] = wrap(me[d] - i, n)
            arrived(slot(buf, at, whole(buf)), ids[p, 1] + i - 1)

    groups = ((0,), (1, 3), (2,))

    def ring(p, stage, s, off):
        buf, order, half = parts[p]
        d = order[stage - 1]
        n = size[d]
        at = {c: (None if c in order[:stage - 1] else me[c]) for c in "xyz"}
        if stage == 3:
            at[order[1]] = wrap(me[order[1]] + off, 4)
        last = s == n // 2
        rows_r = pl.ds(0, half) if last else whole(buf)
        rows_l = pl.ds(half, buf.shape[4] - half) if last else whole(buf)
        return buf, d, n, at, rows_r, rows_l

    def ring_start(p, stage, s, g):
        for off in groups[g]:
            buf, d, n, at, rows_r, rows_l = ring(p, stage, s, off)
            k = take(2)
            ids[p, stage, s, off] = k
            right, left = dict(me), dict(me)
            right[d] = wrap(me[d] + 1, n)
            left[d] = wrap(me[d] - 1, n)
            fwd, back = dict(at), dict(at)
            fwd[d] = wrap(me[d] - (s - 1), n)
            back[d] = wrap(me[d] + (s - 1), n)
            src = slot(buf, fwd, rows_r)
            send(src, src, device(right, core), k)
            src = slot(buf, back, rows_l)
            send(src, src, device(left, core), k + 1)

    def ring_wait(p, stage, s, g):
        for off in groups[g]:
            buf, d, n, at, rows_r, rows_l = ring(p, stage, s, off)
            k = ids[p, stage, s, off]
            fwd, back = dict(at), dict(at)
            fwd[d] = wrap(me[d] - s, n)
            back[d] = wrap(me[d] + s, n)
            arrived(slot(buf, fwd, rows_r), k)
            arrived(slot(buf, back, rows_l), k + 1)

    short = (
        ((), ((2, 1, 0), (3, 1, 0))),
        (((2, 1, 0),), ((2, 2, 0), (3, 1, 1))),
        (((3, 1, 0),), ((3, 2, 0),)),
        (((2, 2, 0),), ((3, 1, 2),)),
        (((3, 1, 1),), ((3, 2, 1),)),
        (((3, 1, 2),), ((3, 2, 2),)),
        (((3, 2, 0), (3, 2, 1), (3, 2, 2)), ()),
    )
    long = short[:3] + (
        short[3],
        short[4],
        (((3, 2, 0),), ((3, 3, 0),)),
        (((3, 1, 2),), ((3, 2, 2),)),
        (((3, 2, 1),), ((3, 3, 1),)),
        (((3, 3, 0),), ((3, 4, 0),)),
        (((3, 2, 2),), ((3, 3, 2),)),
        (((3, 3, 1),), ((3, 4, 1),)),
        (((3, 3, 2),), ((3, 4, 2),)),
        (((3, 4, 0), (3, 4, 1), (3, 4, 2)), ()),
    )
    plan = {"a": short, "b": long, "c": short}

    def pump(p, *events):
        for i in events:
            waits, starts = plan[p][i - 1]
            if i == 1:
                direct_wait(p)
            for w in waits:
                ring_wait(p, *w)
            for w in starts:
                ring_start(p, *w)

    k1a = halo_send(0, 0, 0, 16)
    k1b = halo_send(0, 1, 16, 64)
    for p in "bac":
        direct_start(p)
    k_cov = take(8)
    for g in range(8):
        send(
            cov.at[:, pl.ds(pl.multiple_of((g * 2 + 1 - core) * 1024, 1024), 1024)],
            cmat.at[g, pl.ds(pl.multiple_of(core * 64, 64), 64), :],
            other, k_cov + g,
        )

    has_north = (lat < 15).astype(F32)
    has_south = (lat > 0).astype(F32)

    def stencil(src, step, j, sides):
        l, t = j // 8, lax.rem(j, 8)
        c = src[l, t]
        h = pltpu.roll(sides, 126 - 2 * j, 1)
        e = jnp.where(lane == 127, h, pltpu.roll(c, 127, 1))
        v = jnp.where(lane == 0, h, pltpu.roll(c, 1, 1))
        n = jnp.where(row == 31, has_north * halo_n[step, pl.ds(j, 1), :], pltpu.roll(c, 31, 0))
        s = jnp.where(row == 0, has_south * halo_s[step, pl.ds(j, 1), :], pltpu.roll(c, 1, 0))
        u = src[jnp.minimum(l + 1, 7), t]
        d = src[jnp.maximum(l - 1, 0), t]
        return (
            c + tr[0, l] * (e - c) + tr[1, l] * (v - c) + tr[2, l] * (n - c)
            + tr[3, l] * (s - c) + tr[4, l] * (u - c) + tr[5, l] * (d - c)
        )

    mark("s03_halo1a")
    in_tr.wait()
    sides1a = halo_wait(0, 0, 0, 16, k1a)
    mark("s04_step1a")

    def step_one(sides):
        def body(j, acc):
            v = stencil(adj, 0, j, sides)
            first[j // 8, lax.rem(j, 8)] = v
            return edges(1, j, v, acc)
        return body

    col_s[2] = lax.fori_loop(0, 8, step_one(sides1a), none, unroll=UNROLL)
    k2a = halo_send(1, 0, 0, 8)
    mark("s05_step1a2")
    rest1 = lax.fori_loop(8, 16, step_one(sides1a), none, unroll=UNROLL)
    mark("s06_pump")
    pump("b", 1)
    mark("s07_halo1b")
    sides1b = halo_wait(0, 1, 16, 64, k1b)
    mark("s08_step1b")
    col_s[3] = lax.fori_loop(16, 64, step_one(sides1b), rest1, unroll=UNROLL)
    k2b = halo_send(1, 1, 8, 64)
    mark("s09_pump")
    pump("b", 2)
    pump("a", 1)
    pump("c", 1)
    mark("s10_halo2a")
    sides2a = halo_wait(1, 0, 0, 8, k2a)
    mark("s11_step2a")

    def step_two(sides):
        def body(j, acc):
            v = stencil(first, 1, j, sides)
            aout[lax.rem(j, 8), j // 8] = v
            return jnp.where(lane == j, jnp.sum(v, axis=1, keepdims=True), acc)
        return body

    sums = lax.fori_loop(0, 8, step_two(sides2a), none, unroll=UNROLL)
    lane8 = lax.broadcasted_iota(jnp.int32, (8, 128), 1)
    row8 = lax.broadcasted_iota(jnp.int32, (8, 128), 0)
    tight = sums[0:8]
    for i in range(1, 4):
        tight = jnp.where(lane8 // 8 == i, pltpu.roll(sums[8 * i:8 * i + 8], 8 * i, 1), tight)
    ybar[lon] = tight
    kz = take(15)
    for i in range(1, 16):
        send(ybar.at[lon], ybar.at[lon], (lat, wrap(lon + i, 16)), kz + i - 1)
    mark("s12_pump")
    pump("b", 3)
    pump("b", 4)
    mark("s13_halo2b")
    sides2b = halo_wait(1, 1, 8, 64, k2b)
    mark("s14_step2b")
    sums = lax.fori_loop(8, 64, step_two(sides2b), none, unroll=UNROLL)
    lane16 = lax.broadcasted_iota(jnp.int32, (16, 128), 1)
    row16 = lax.broadcasted_iota(jnp.int32, (16, 128), 0)
    zbuf[lon] = jnp.where(lane16 < 64, sums[0:16], pltpu.roll(sums[16:32], 64, 1))
    kw = take(15)
    for i in range(1, 16):
        send(zbuf.at[lon], zbuf.at[lon], (lat, wrap(lon + i, 16)), kw + i - 1)
    mark("s15_pump")
    pump("a", 2)
    pump("c", 2)
    pump("b", 5)
    pump("b", 6)
    for c in in_late:
        c.wait()
    flags = 0.5 * jnp.sum(
        jnp.where(lane == row, jnp.broadcast_to(polar[...], (32, 128)), 0).astype(F32), axis=1, keepdims=True
    )
    lane256 = lax.broadcasted_iota(jnp.int32, (256, 128), 1)
    row256 = lax.broadcasted_iota(jnp.int32, (256, 128), 0)
    mine_at = jnp.sum(
        jnp.where(lane256 == number - lanes_at, tiles[...] - 64 * number, 0).astype(F32), axis=1, keepdims=True
    )
    spread = jnp.where(lane256 // 8 == lax.rem(row256, 16), mine_at, 0.0).astype(BF16)
    pick = (
        lax.broadcasted_iota(jnp.int32, (16, 256), 1) // 16 == lax.broadcasted_iota(jnp.int32, (16, 256), 0)
    ).astype(F32).astype(BF16)
    reg = dot(pick, spread).astype(jnp.int32)
    mark("s16_zwait")
    for i in range(1, 16):
        arrived(ybar.at[wrap(lon - i, 16)], kz + i - 1)
    mark("s17_surf")
    total = ybar[0]
    for i in range(1, 16):
        total = total + ybar[i]
    total = total * (1.0 / 2048.0)
    mean0 = jnp.concatenate([total] + [pltpu.roll(total, 128 - 8 * i, 1) for i in range(1, 4)], axis=0)

    def filtered(j, mean):
        v = aout[lax.rem(j, 8), j // 8]
        v = v + flags * (jnp.sum(jnp.where(lane == j, mean, 0.0), axis=1, keepdims=True) - v)
        aout[lax.rem(j, 8), j // 8] = v
        return v

    for t in range(8):
        surf[t] = filtered(t, mean0) * weight[...]

    mark("s18_pump")
    pump("a", 3)
    pump("c", 3)
    pump("b", 7)
    mark("s19_regions")

    sub8 = lax.broadcasted_iota(jnp.int32, (16, 128), 0)

    def regions(r, acc):
        lhs, rhs = [], [[], [], []]
        for h in range(2):
            i = 2 * r + h
            local = rl[pl.ds(i, 1), :]
            low = jnp.broadcast_to(local & 15, (16, 128))
            high = jnp.broadcast_to(local >> 4, (8, 128))
            lhs.append((low == sub8).astype(F32).astype(BF16))
            s = jnp.concatenate([surf[t, pl.ds(i, 1), :] for t in range(8)], axis=0)
            for n in range(3):
                piece = s.astype(BF16).astype(F32)
                s = s - piece
                rhs[n].append(
                    jnp.concatenate([jnp.where(high == a, piece, 0.0) for a in range(16)], axis=0).astype(BF16)
                )
        left = jnp.concatenate(lhs, axis=1)
        for n in range(3):
            acc = acc + dot_nt(left, jnp.concatenate(rhs[n], axis=1))
        return acc

    m = lax.fori_loop(0, 16, regions, jnp.zeros((16, 128), F32), unroll=2)
    for i in range(16):
        mbuf[i] = m[i:i + 1, :]
    xbuf[lon] = mbuf[lon]
    kx = take(15)
    for i in range(1, 16):
        to = wrap(lon + i, 16)
        send(mbuf.at[to], xbuf.at[lon], (lat, to), kx + i - 1)

    mark("s20_pump")
    pump("a", 4)
    pump("c", 4)
    pump("b", 8)
    pump("b", 9)
    mark("s21_rest")
    for i in range(1, 16):
        arrived(zbuf.at[wrap(lon - i, 16)], kw + i - 1)
    total = zbuf[0]
    for i in range(1, 16):
        total = total + zbuf[i]
    total = total * (1.0 / 2048.0)
    mean = jnp.concatenate([total, pltpu.roll(total, 64, 1)], axis=0)

    def rest(j, carry):
        filtered(j, mean)
        return carry

    lax.fori_loop(8, 64, rest, 0, unroll=UNROLL)
    out_field = load(aout, aout_h, 18)
    mark("s22_pump")
    pump("a", 5)
    pump("c", 5)
    pump("b", 10)
    pump("b", 11)
    mark("s23_xwait")
    for i in range(1, 16):
        arrived(xbuf.at[wrap(lon - i, 16)], kx + i - 1)
    mark("s24_turn")
    got = jnp.concatenate([xbuf[i] for i in range(16)], axis=0)
    turned = jnp.zeros((16, 128), F32)
    group = lane16 // 8
    for d in range(16):
        moved = got if d == 0 else pltpu.roll(pltpu.roll(got, 16 - d, 0), 8 * d, 1)
        turned = jnp.where(lax.rem(group - row16 + 16, 16) == d, moved, turned)
    for i in range(16):
        ybuf[i] = turned[i:i + 1, :]
    obuf[lat] = ybuf[lat]
    ky = take(15)
    for i in range(1, 16):
        to = wrap(lat + i, 16)
        send(ybuf.at[to], obuf.at[lat], (to, lon), ky + i - 1)
    mark("s25_pump")
    pump("a", 6)
    pump("c", 6)
    pump("b", 12)
    mark("s26_owait")
    for i in range(1, 16):
        arrived(obuf.at[wrap(lat - i, 16)], ky + i - 1)

    mark("s27_fresh")
    packed = jnp.zeros((8, 128), F32)
    for v in range(8):
        f = jnp.zeros((8, 128), F32)
        for a in range(16):
            f = f + jnp.where(reg[a:a + 1, :] == row8 + 8 * v, obuf[a], 0.0)
        for shift in (64, 32, 16, 8):
            f = f + pltpu.roll(f, shift, 1)
        packed = jnp.where(lane8 // 8 == v, f, packed)
    fr[y, xl, z, xh] = packed.astype(BF16).astype(F32)
    kf = take(15)
    for i in range(1, 16):
        here = fr.at[y, xl, z, xh]
        send(here, here, (lat, wrap(lon + i, 16)), kf + i - 1)
    mark("s28_pump")
    mark("s29_fwait")
    for i in range(1, 16):
        o = wrap(lon - i, 16)
        arrived(fr.at[y, xl, o // 2, lax.rem(o, 2)], kf + i - 1)
    kg = take(7)
    for i in range(1, 8):
        g = wrap(lat // 2 + i, 8)
        send(fr.at[y, xl], fr.at[y, xl], (g * 2 + core, lon), kg + i - 1)
    mark("s30_pump")
    pump("a", 7)
    pump("c", 7)
    pump("b", 13)
    for c in own_cov:
        c.wait()
    for g in range(8):
        arrived(cmat.at[g, pl.ds(pl.multiple_of((1 - core) * 64, 64), 64), :], k_cov + g)

    mark("s31_product")
    pacc[...] = jnp.zeros((2, 64, 512), F32)

    def product(g, carry):
        gy, gx = g // 2, lax.rem(g, 2)
        c = cmat[g]
        r0 = jnp.concatenate(
            [b0[gy, gx][:, :, 0:64].reshape(1024, 128), b1[gy, gx].reshape(1024, 128)], axis=1
        )
        left = dot(c, r0)
        pacc[0, :, 0:256] += left[0:64]
        pacc[1, :, 0:256] += left[64:128]
        tails = b0[gy, gx][:, :, 64:80].reshape(256, 128)
        pieces = []
        for q in range(4):
            sel = (
                lax.broadcasted_iota(jnp.int32, (128, 128), 0)
                == lax.broadcasted_iota(jnp.int32, (128, 128), 1) + 32 * q
            ).astype(F32).astype(BF16)
            pieces.append(dot(tails, sel).astype(BF16).reshape(16, 16, 128))
        last = jnp.concatenate(pieces, axis=1).reshape(1024, 128)
        right = dot(c, jnp.concatenate([b2[gy, gx].reshape(1024, 128), last], axis=1))
        pacc[0, :, 256:512] += right[0:64]
        pacc[1, :, 256:512] += right[64:128]
        return carry

    lax.fori_loop(0, 8, product, 0)
    kp = take()
    send(pacc.at[1 - core], precv, other, kp)

    mark("s32_f2wait")
    for i in range(1, 8):
        g = wrap(lat // 2 - i, 8)
        arrived(fr.at[g // 2, lax.rem(g, 2)], kg + i - 1)

    mark("s33_freshprod")

    def fresh_product(g, acc):
        f = fr[g // 2, lax.rem(g, 2)].reshape(16, 8, 128)
        lanes = lax.broadcasted_iota(jnp.int32, (16, 8, 128), 2) // 8
        w = jnp.concatenate([jnp.where(lanes == v, f, 0.0) for v in range(8)], axis=1)
        return acc + dot(cmat[g], w.astype(BF16).reshape(1024, 128))

    added = lax.fori_loop(0, 8, fresh_product, jnp.zeros((128, 128), F32))
    for shift in (64, 32, 16, 8):
        added = added + pltpu.roll(added, shift, 1)
    aacc[0] = added[0:64]
    aacc[1] = added[64:128]
    mark("s34_exch")
    ka = take()
    send(aacc.at[1 - core], arecv, other, ka)
    arrived(precv, kp)
    arrived(arecv, ka)
    mark("s35_final")
    mine = aacc[core] + arecv[...]
    base = pacc[core] + precv[...]
    for n in range(4):
        week_of = (lax.broadcasted_iota(jnp.int32, (64, 128), 1) + 128 * n) // 8
        pre[:, 128 * n:128 * n + 128] = base[:, 128 * n:128 * n + 128] + jnp.where(
            week_of == jnp.broadcast_to(week[...], (64, 128)), mine, 0.0
        )
    out_pre = load(pre, pre_h, 19)
    for c in sends:
        c.wait_send()
    out_field.wait()
    out_pre.wait()
    mark("")


COPIES = 240
UNROLL = 4
PROFILE = False


def shards(adjoint, transport, cell_weight, region_local, tile_regions, polar_rows, week_index, grad_in, covariance):
    hbm = pl.BlockSpec(memory_space=pl.ANY)
    aout, pre = pl.pallas_call(
        kernel,
        out_shape=(
            jax.ShapeDtypeStruct((8, 8, 32, 128), F32),
            jax.ShapeDtypeStruct((64, 512), F32),
        ),
        in_specs=[hbm] * 9,
        out_specs=(hbm, hbm),
        scratch_shapes=[
            pltpu.VMEM((8, 8, 32, 128), F32),
            pltpu.VMEM((6, 8, 32, 128), F32),
            pltpu.VMEM((32, 128), F32),
            pltpu.VMEM((32, 128), jnp.int32),
            pltpu.VMEM((256, 128), jnp.int32),
            pltpu.VMEM((1, 128), jnp.int32),
            pltpu.VMEM((1, 128), jnp.int32),
            pltpu.VMEM((64, 416), BF16),
            pltpu.VMEM((8, 8, 32, 128), F32),
            pltpu.VMEM((8, 32, 128), F32),
            pltpu.VMEM((4, 2, 8, 2, 80, 128), BF16),
            pltpu.VMEM((4, 2, 8, 2, 64, 128), BF16),
            pltpu.VMEM((4, 2, 8, 2, 64, 128), BF16),
            pltpu.VMEM((8, 128, 1024), BF16),
            pltpu.VMEM((4, 2, 8, 2, 8, 128), F32),
            pltpu.VMEM((4, 32, 128), F32),
            pltpu.VMEM((2, 64, 128), F32),
            pltpu.VMEM((2, 64, 128), F32),
            pltpu.VMEM((4, 32, 128), F32),
            pltpu.VMEM((4, 32, 128), F32),
            pltpu.VMEM((2, 64, 128), F32),
            pltpu.VMEM((2, 64, 128), F32),
            pltpu.VMEM((16, 16, 128), F32),
            pltpu.VMEM((16, 8, 128), F32),
            pltpu.VMEM((16, 1, 128), F32),
            pltpu.VMEM((16, 1, 128), F32),
            pltpu.VMEM((16, 1, 128), F32),
            pltpu.VMEM((16, 1, 128), F32),
            pltpu.VMEM((2, 64, 512), F32),
            pltpu.VMEM((64, 512), F32),
            pltpu.VMEM((2, 64, 128), F32),
            pltpu.VMEM((64, 128), F32),
            pltpu.VMEM((8, 8, 32, 128), F32),
            pltpu.VMEM((64, 512), F32),
            pltpu.SemaphoreType.DMA((COPIES,)),
            pltpu.SemaphoreType.DMA((COPIES,)),
            pltpu.SemaphoreType.DMA((8,)),
            pltpu.SemaphoreType.DMA((20,)),
        ],
        compiler_params=pltpu.CompilerParams(
            collective_id=0, has_side_effects=True, vmem_limit_bytes=67043328
        ),
        name="window",
    )(
        adjoint, transport, cell_weight, region_local, tile_regions,
        jnp.pad(polar_rows, (0, 96)).reshape(1, 128),
        jnp.broadcast_to(week_index.reshape(1, 1), (1, 128)), grad_in, covariance,
    )
    return aout, pre[:, :416]


def solution(mesh):
    both = ("lat", "lon")
    return jax.shard_map(
        shards,
        mesh=mesh,
        in_specs=(
            P(None, None, "lat", "lon"), P(None, None, "lat", "lon"), P("lat", "lon"), P("lat", "lon"),
            P(), P("lat"), P(), P(both, None), P(both, None),
        ),
        out_specs=(P(None, None, "lat", "lon"), P(both, None)),
        check_vma=False,
    )
```

time: 96.5 us -> 79.2 us (0.82)
  Pallas kernels: 84.9 us -> 73.1 us
  local copies, waits for them, and re-layouts: 8.15 us -> 4.64 us
  other arithmetic: 1.75 us -> 0 us
    pallas_call x1, Pallas kernels: 84.9 us -> 73.1 us  [shards(): pl.pallas_call(kernel, out_shape=(jax.ShapeDtypeStruct((8, 8, 32, 128), F...]
    unnamed x14 -> x4, local copies, waits for them, and re-layouts: 7.87 us -> 2.96 us
    reshape x2 -> x1, local copies, waits for them, and re-layouts: 0.06 us -> 1.17 us  [shards(): jnp.pad(polar_rows, (0, 96)).reshape(1, 128)]
    sub x1 -> x0, other arithmetic: 1.08 us -> none  [shards(): lax.dynamic_slice_in_dim(tile_regions, me, 1, axis=1).reshape(16, 16)]
where the time goes in v2:
time: 79.2 us; the launch traced here: 79.1 us
  Pallas kernels  73.1 us (92%)
  local copies, waits for them, and re-layouts  4.64 us (6%)
  between operations  1.29 us (2%)
    pallas_call x1, Pallas kernels, shards(): pl.pallas_call(kernel, out_shape=(jax.ShapeDtypeStruct((8, 8, 32, 128), F...  73.1 us
    unnamed x4, local copies, waits for them, and re-layouts  2.96 us

profile of v2, /device:TPU:1, one launch (start us, length us, event | category | flops | bytes accessed | tf_op | source)
XLA Modules:
  0.0 79.1 jit_solution(14873450704240614565)
XLA Ops:
  1.3 0.5 broadcast_in_dim.8.week_h
  1.8 1.2 %pad_bitcast_fusion.polar_h = s32[1,128]{1,0:T(1,128)} fusion(s32[32]{0:T(128)} %param.14), kind=kLoop, calls=%fused_computation | loop fusion | bytes 640 | tf_op jit(solution)/shard_map/reshape | solution.py:665
  3.0 73.1 %window.1 = (f32[8,8,32,128]{3,2,1,0:T(8,128)}, f32[64,512]{1,0:T(8,128)}) custom-call(f32[8,8,32,128]{3,2,1,0:T(8,128)} %adj_h.1, f32[6,8,32,128]{3,2,1,0:T(8,128)} %tr_h.1, f32[32,128]{1,0:T(8,128)} %weight_h.1, s32[32,128]{1,0:T(8,128)} %rl_h.1, s32[256,256]{1,0:T(8,128)} %tiles_h.1, s32[1,128]{1,0:T(1,128)} %pad_bitcast_fusion.polar_h, ...), custom_call_target="tpu_custom_call" | custom-call | tf_op jit(solution)/shard_map/window/pallas_call | solution.py:611
  76.1 0.0 copy-start
  76.1 2.3 %copy.14 = f32[8,8,32,128]{3,2,1,0:T(8,128)} copy(f32[8,8,32,128]{3,2,1,0:T(8,128)} %get-tuple-element.8) | data formatting | bytes 2097152
  78.4 0.0 copy-done
  78.4 0.7 copy.15
Async XLA Ops:
  76.1 2.3 %copy-start = (f32[64,512]{1,0:T(8,128)S(1)}, f32[64,512]{1,0:T(8,128)}, u32[]{:S(2)}) copy-start(f32[64,512]{1,0:T(8,128)} %get-tuple-element.5) | copy-start | bytes 393220

commit v3 on v2

--- a/solution.py
+++ b/solution.py
@@ -55,17 +55,17 @@
         )
 
     def send(src, dst, to, k):
-        c = remote(src, dst, to, k)
-        c.start()
-        sends.append(c)
-
-    def take(count=1):
+        remote(src, dst, to, k).start()
+
+    def take(*sizes):
         k = counter[0]
-        counter[0] += count
+        counter[0] += len(sizes)
+        for i, view in enumerate(sizes):
+            sends.append((view, k + i))
         return k
 
-    def arrived(dst, k):
-        remote(dst, dst, (lat, lon), k).wait_recv()
+    def arrived(view, k):
+        remote(view, view, (lat, lon), k).wait_recv()
 
     other = (lat + 1 - 2 * core, lon)
 
@@ -107,15 +107,13 @@
         load(weight_h, weight, 13), load(rl_h, rl, 14), load(polar_h, polar, 15),
         load(tiles_h.at[:, pl.ds(lanes_at, 128)], tiles, 16), load(week_h, week, 17),
     ]
-    own_cov = []
     for g in range(8):
         c = pltpu.make_async_copy(
             cov.at[:, pl.ds(pl.multiple_of((g * 2 + core) * 1024, 1024), 1024)],
             cmat.at[g, pl.ds(pl.multiple_of(core * 64, 64), 64), :],
-            lsem.at[g],
+            lsem.at[0],
         )
         c.start()
-        own_cov.append(c)
 
     lane = lax.broadcasted_iota(jnp.int32, (32, 128), 1)
     row = lax.broadcasted_iota(jnp.int32, (32, 128), 0)
@@ -132,21 +130,6 @@
     in_adj[0].wait()
     in_adj[1].wait()
     col_s[0] = lax.fori_loop(0, 16, pack, none, unroll=4)
-    for c in in_adj[2:]:
-        c.wait()
-    col_s[1] = lax.fori_loop(16, 64, pack, none, unroll=4)
-
-    for c in in_grad:
-        c.wait()
-    tail = jnp.zeros((16, 128), F32)
-    for q in range(4):
-        sel = (
-            lax.broadcasted_iota(jnp.int32, (32, 128), 1)
-            == lax.broadcasted_iota(jnp.int32, (32, 128), 0) + 32 * q
-        ).astype(F32).astype(BF16)
-        tail = tail + dot(gtail[16 * q:16 * q + 16, 384:416], sel)
-    b0[y, xl, z, xh, 64:80, :] = tail.astype(BF16)
-
     mark("s01_barrier")
     pl.semaphore_wait(barrier, 31)
     mark("s02_send1")
@@ -155,8 +138,9 @@
     north, south = wrap(lat + 1, 16), wrap(lat - 1, 16)
 
     def halo_send(s, i, lo, hi):
-        k = take(4)
         rows = pl.ds(lo, hi - lo)
+        cols = col_s.at[2 * s + i]
+        k = take(cols, cols, row_n.at[s, rows], row_n.at[s, rows])
         send(row_n.at[s, rows], halo_s.at[s, rows], (north, lon), k + 2)
         send(row_s.at[s, rows], halo_n.at[s, rows], (south, lon), k + 3)
         send(col_s.at[2 * s + i], col_w.at[2 * s + i], (lat, east), k)
@@ -174,7 +158,7 @@
     parts = {
         "a": (b0, "zyx", 48),
         "b": (b1, "yxz", 32),
-        "c": (b2, "zxy", 32),
+        "c": (b2, "xzy", 32),
     }
 
     def slot(buf, at, rows):
@@ -189,28 +173,36 @@
 
     ids = {}
 
+    singles = {"a": b0.at[0, 0, 0:7, 0], "b": b1.at[0:3, 0, 0, 0], "c": b2.at[0, 0, 0:3, 0]}
+    views = {
+        "a": {1: b0.at[0, 0, :, 0], 2: b0.at[0, 0], 4: b0.at[0]},
+        "b": {1: b1.at[:, 0, 0, 0], 2: b1.at[:, 0, 0], 4: b1.at[:, :, 0]},
+        "c": {1: b2.at[0, :, 0], 2: b2.at[0, 0, 0:4], 4: b2.at[0, 0]},
+    }
+
     def direct_start(p):
         buf, order, _ = parts[p]
         d = order[0]
         n = size[d]
-        k = take(n - 1)
+        k = take(singles[p])
         ids[p, 1] = k
         for i in range(1, n):
             to = dict(me)
             to[d] = wrap(me[d] + i, n)
             here = slot(buf, me, whole(buf))
-            send(here, here, device(to, core), k + i - 1)
+            send(here, here, device(to, core), k)
 
     def direct_wait(p):
-        buf, order, _ = parts[p]
-        d = order[0]
-        n = size[d]
-        for i in range(1, n):
-            at = dict(me)
-            at[d] = wrap(me[d] - i, n)
-            arrived(slot(buf, at, whole(buf)), ids[p, 1] + i - 1)
-
-    groups = ((0,), (1, 3), (2,))
+        arrived(singles[p], ids[p, 1])
+
+    groups = {4: ((0,), (1, 3), (2,)), 8: ((0,), (1, 7), (2, 6), (3, 5), (4,))}
+
+    def offsets(p, stage, g):
+        return groups[size[parts[p][1][1]]][g] if stage == 3 else (0,)
+
+    def unit(p, stage, s, g):
+        n = size[parts[p][1][stage - 1]]
+        return views[p][len(offsets(p, stage, g)) * (1 if s == n // 2 else 2)]
 
     def ring(p, stage, s, off):
         buf, order, half = parts[p]
@@ -218,17 +210,17 @@
         n = size[d]
         at = {c: (None if c in order[:stage - 1] else me[c]) for c in "xyz"}
         if stage == 3:
-            at[order[1]] = wrap(me[order[1]] + off, 4)
+            at[order[1]] = wrap(me[order[1]] + off, size[order[1]])
         last = s == n // 2
         rows_r = pl.ds(0, half) if last else whole(buf)
         rows_l = pl.ds(half, buf.shape[4] - half) if last else whole(buf)
         return buf, d, n, at, rows_r, rows_l
 
     def ring_start(p, stage, s, g):
-        for off in groups[g]:
+        k = take(unit(p, stage, s, g))
+        ids[p, stage, s, g] = k
+        for off in offsets(p, stage, g):
             buf, d, n, at, rows_r, rows_l = ring(p, stage, s, off)
-            k = take(2)
-            ids[p, stage, s, off] = k
             right, left = dict(me), dict(me)
             right[d] = wrap(me[d] + 1, n)
             left[d] = wrap(me[d] - 1, n)
@@ -238,17 +230,10 @@
             src = slot(buf, fwd, rows_r)
             send(src, src, device(right, core), k)
             src = slot(buf, back, rows_l)
-            send(src, src, device(left, core), k + 1)
+            send(src, src, device(left, core), k)
 
     def ring_wait(p, stage, s, g):
-        for off in groups[g]:
-            buf, d, n, at, rows_r, rows_l = ring(p, stage, s, off)
-            k = ids[p, stage, s, off]
-            fwd, back = dict(at), dict(at)
-            fwd[d] = wrap(me[d] - s, n)
-            back[d] = wrap(me[d] + s, n)
-            arrived(slot(buf, fwd, rows_r), k)
-            arrived(slot(buf, back, rows_l), k + 1)
+        arrived(unit(p, stage, s, g), ids[p, stage, s, g])
 
     short = (
         ((), ((2, 1, 0), (3, 1, 0))),
@@ -271,7 +256,20 @@
         (((3, 3, 2),), ((3, 4, 2),)),
         (((3, 4, 0), (3, 4, 1), (3, 4, 2)), ()),
     )
-    plan = {"a": short, "b": long, "c": short}
+    other_way = (
+        ((), ((2, 1, 0), (3, 1, 0))),
+        (((2, 1, 0),), ((2, 2, 0), (3, 1, 1))),
+        (((3, 1, 0),), ((3, 2, 0),)),
+        (((2, 2, 0),), ((2, 3, 0), (3, 1, 2))),
+        (((3, 1, 1),), ((3, 2, 1),)),
+        (((2, 3, 0),), ((2, 4, 0), (3, 1, 3))),
+        (((3, 1, 2),), ((3, 2, 2),)),
+        (((2, 4, 0),), ((3, 1, 4),)),
+        (((3, 1, 3),), ((3, 2, 3),)),
+        (((3, 1, 4),), ((3, 2, 4),)),
+        (((3, 2, 0), (3, 2, 1), (3, 2, 2), (3, 2, 3), (3, 2, 4)), ()),
+    )
+    plan = {"a": short, "b": long, "c": other_way}
 
     def pump(p, *events):
         for i in events:
@@ -284,15 +282,30 @@
                 ring_start(p, *w)
 
     k1a = halo_send(0, 0, 0, 16)
+    for c in in_adj[2:]:
+        c.wait()
+    col_s[1] = lax.fori_loop(16, 64, pack, none, unroll=4)
+
+    for c in in_grad:
+        c.wait()
+    tail = jnp.zeros((16, 128), F32)
+    for q in range(4):
+        sel = (
+            lax.broadcasted_iota(jnp.int32, (32, 128), 1)
+            == lax.broadcasted_iota(jnp.int32, (32, 128), 0) + 32 * q
+        ).astype(F32).astype(BF16)
+        tail = tail + dot(gtail[16 * q:16 * q + 16, 384:416], sel)
+    b0[y, xl, z, xh, 64:80, :] = tail.astype(BF16)
+
     k1b = halo_send(0, 1, 16, 64)
     for p in "bac":
         direct_start(p)
-    k_cov = take(8)
+    k_cov = take(cmat.at[:, 0:64])
     for g in range(8):
         send(
             cov.at[:, pl.ds(pl.multiple_of((g * 2 + 1 - core) * 1024, 1024), 1024)],
             cmat.at[g, pl.ds(pl.multiple_of(core * 64, 64), 64), :],
-            other, k_cov + g,
+            other, k_cov,
         )
 
     has_north = (lat < 15).astype(F32)
@@ -331,15 +344,16 @@
     rest1 = lax.fori_loop(8, 16, step_one(sides1a), none, unroll=UNROLL)
     mark("s06_pump")
     pump("b", 1)
+    pump("c", 1)
     mark("s07_halo1b")
     sides1b = halo_wait(0, 1, 16, 64, k1b)
     mark("s08_step1b")
     col_s[3] = lax.fori_loop(16, 64, step_one(sides1b), rest1, unroll=UNROLL)
     k2b = halo_send(1, 1, 8, 64)
     mark("s09_pump")
+    pump("a", 1)
     pump("b", 2)
-    pump("a", 1)
-    pump("c", 1)
+    pump("c", 2)
     mark("s10_halo2a")
     sides2a = halo_wait(1, 0, 0, 8, k2a)
     mark("s11_step2a")
@@ -358,31 +372,22 @@
     for i in range(1, 4):
         tight = jnp.where(lane8 // 8 == i, pltpu.roll(sums[8 * i:8 * i + 8], 8 * i, 1), tight)
     ybar[lon] = tight
-    kz = take(15)
+    kz = take(ybar.at[0:15])
     for i in range(1, 16):
-        send(ybar.at[lon], ybar.at[lon], (lat, wrap(lon + i, 16)), kz + i - 1)
+        send(ybar.at[lon], ybar.at[lon], (lat, wrap(lon + i, 16)), kz)
     mark("s12_pump")
     pump("b", 3)
+    pump("c", 3)
+    mark("s15_pump")
     pump("b", 4)
-    mark("s13_halo2b")
-    sides2b = halo_wait(1, 1, 8, 64, k2b)
-    mark("s14_step2b")
-    sums = lax.fori_loop(8, 64, step_two(sides2b), none, unroll=UNROLL)
-    lane16 = lax.broadcasted_iota(jnp.int32, (16, 128), 1)
-    row16 = lax.broadcasted_iota(jnp.int32, (16, 128), 0)
-    zbuf[lon] = jnp.where(lane16 < 64, sums[0:16], pltpu.roll(sums[16:32], 64, 1))
-    kw = take(15)
-    for i in range(1, 16):
-        send(zbuf.at[lon], zbuf.at[lon], (lat, wrap(lon + i, 16)), kw + i - 1)
-    mark("s15_pump")
-    pump("a", 2)
-    pump("c", 2)
-    pump("b", 5)
-    pump("b", 6)
+    pump("c", 4)
     for c in in_late:
         c.wait()
     flags = 0.5 * jnp.sum(
-        jnp.where(lane == row, jnp.broadcast_to(polar[...], (32, 128)), 0).astype(F32), axis=1, keepdims=True
+        jnp.where(
+            lax.broadcasted_iota(jnp.int32, (32, 32), 0) == lax.broadcasted_iota(jnp.int32, (32, 32), 1),
+            jnp.broadcast_to(polar[...], (32, 32)), 0,
+        ).astype(F32), axis=1, keepdims=True
     )
     lane256 = lax.broadcasted_iota(jnp.int32, (256, 128), 1)
     row256 = lax.broadcasted_iota(jnp.int32, (256, 128), 0)
@@ -395,8 +400,7 @@
     ).astype(F32).astype(BF16)
     reg = dot(pick, spread).astype(jnp.int32)
     mark("s16_zwait")
-    for i in range(1, 16):
-        arrived(ybar.at[wrap(lon - i, 16)], kz + i - 1)
+    arrived(ybar.at[0:15], kz)
     mark("s17_surf")
     total = ybar[0]
     for i in range(1, 16):
@@ -414,9 +418,9 @@
         surf[t] = filtered(t, mean0) * weight[...]
 
     mark("s18_pump")
-    pump("a", 3)
-    pump("c", 3)
-    pump("b", 7)
+    pump("a", 2)
+    pump("b", 5)
+    pump("c", 5)
     mark("s19_regions")
 
     sub8 = lax.broadcasted_iota(jnp.int32, (16, 128), 0)
@@ -445,39 +449,30 @@
     for i in range(16):
         mbuf[i] = m[i:i + 1, :]
     xbuf[lon] = mbuf[lon]
-    kx = take(15)
+    kx = take(xbuf.at[0:15])
     for i in range(1, 16):
         to = wrap(lon + i, 16)
-        send(mbuf.at[to], xbuf.at[lon], (lat, to), kx + i - 1)
-
+        send(mbuf.at[to], xbuf.at[lon], (lat, to), kx)
+
+    mark("s13_halo2b")
+    sides2b = halo_wait(1, 1, 8, 64, k2b)
+    mark("s14_step2b")
+    sums = lax.fori_loop(8, 64, step_two(sides2b), none, unroll=UNROLL)
+    lane16 = lax.broadcasted_iota(jnp.int32, (16, 128), 1)
+    row16 = lax.broadcasted_iota(jnp.int32, (16, 128), 0)
+    zbuf[lon] = jnp.where(lane16 < 64, sums[0:16], pltpu.roll(sums[16:32], 64, 1))
+    kw = take(zbuf.at[0:15])
+    for i in range(1, 16):
+        send(zbuf.at[lon], zbuf.at[lon], (lat, wrap(lon + i, 16)), kw)
     mark("s20_pump")
-    pump("a", 4)
-    pump("c", 4)
-    pump("b", 8)
-    pump("b", 9)
-    mark("s21_rest")
-    for i in range(1, 16):
-        arrived(zbuf.at[wrap(lon - i, 16)], kw + i - 1)
-    total = zbuf[0]
-    for i in range(1, 16):
-        total = total + zbuf[i]
-    total = total * (1.0 / 2048.0)
-    mean = jnp.concatenate([total, pltpu.roll(total, 64, 1)], axis=0)
-
-    def rest(j, carry):
-        filtered(j, mean)
-        return carry
-
-    lax.fori_loop(8, 64, rest, 0, unroll=UNROLL)
-    out_field = load(aout, aout_h, 18)
+    pump("b", 6)
+    pump("c", 6)
+    pump("a", 3)
+    pump("b", 7)
+    pump("c", 7)
     mark("s22_pump")
-    pump("a", 5)
-    pump("c", 5)
-    pump("b", 10)
-    pump("b", 11)
     mark("s23_xwait")
-    for i in range(1, 16):
-        arrived(xbuf.at[wrap(lon - i, 16)], kx + i - 1)
+    arrived(xbuf.at[0:15], kx)
     mark("s24_turn")
     got = jnp.concatenate([xbuf[i] for i in range(16)], axis=0)
     turned = jnp.zeros((16, 128), F32)
@@ -488,17 +483,34 @@
     for i in range(16):
         ybuf[i] = turned[i:i + 1, :]
     obuf[lat] = ybuf[lat]
-    ky = take(15)
+    ky = take(obuf.at[0:15])
     for i in range(1, 16):
         to = wrap(lat + i, 16)
-        send(ybuf.at[to], obuf.at[lat], (to, lon), ky + i - 1)
+        send(ybuf.at[to], obuf.at[lat], (to, lon), ky)
     mark("s25_pump")
-    pump("a", 6)
-    pump("c", 6)
-    pump("b", 12)
+    pump("a", 4)
+    pump("b", 8)
+    pump("c", 8)
+    pump("b", 9)
+    mark("s21_rest")
+    arrived(zbuf.at[0:15], kw)
+    total = zbuf[0]
+    for i in range(1, 16):
+        total = total + zbuf[i]
+    total = total * (1.0 / 2048.0)
+    mean = jnp.concatenate([total, pltpu.roll(total, 64, 1)], axis=0)
+
+    def rest(j, carry):
+        filtered(j, mean)
+        return carry
+
+    lax.fori_loop(8, 64, rest, 0, unroll=UNROLL)
+    out_field = load(aout, aout_h, 18)
     mark("s26_owait")
-    for i in range(1, 16):
-        arrived(obuf.at[wrap(lat - i, 16)], ky + i - 1)
+    pump("a", 5)
+    pump("c", 9)
+    pump("b", 10)
+    arrived(obuf.at[0:15], ky)
 
     mark("s27_fresh")
     packed = jnp.zeros((8, 128), F32)
@@ -509,28 +521,29 @@
         for shift in (64, 32, 16, 8):
             f = f + pltpu.roll(f, shift, 1)
         packed = jnp.where(lane8 // 8 == v, f, packed)
-    fr[y, xl, z, xh] = packed.astype(BF16).astype(F32)
-    kf = take(15)
+    packed = packed.astype(BF16).astype(F32)
+    fr[y, xl, z, xh] = packed[0:4] + pltpu.roll(packed[4:8], 64, 1)
+    kf = take(fr.at[0:3, 0, 0:5, 0])
     for i in range(1, 16):
         here = fr.at[y, xl, z, xh]
-        send(here, here, (lat, wrap(lon + i, 16)), kf + i - 1)
+        send(here, here, (lat, wrap(lon + i, 16)), kf)
     mark("s28_pump")
+    pump("a", 6)
+    pump("c", 10)
+    pump("b", 11)
+    pump("b", 12)
     mark("s29_fwait")
-    for i in range(1, 16):
-        o = wrap(lon - i, 16)
-        arrived(fr.at[y, xl, o // 2, lax.rem(o, 2)], kf + i - 1)
-    kg = take(7)
+    arrived(fr.at[0:3, 0, 0:5, 0], kf)
+    kg = take(fr.at[:, :, 0:7])
     for i in range(1, 8):
         g = wrap(lat // 2 + i, 8)
-        send(fr.at[y, xl], fr.at[y, xl], (g * 2 + core, lon), kg + i - 1)
+        send(fr.at[y, xl], fr.at[y, xl], (g * 2 + core, lon), kg)
     mark("s30_pump")
     pump("a", 7)
-    pump("c", 7)
+    pump("c", 11)
     pump("b", 13)
-    for c in own_cov:
-        c.wait()
-    for g in range(8):
-        arrived(cmat.at[g, pl.ds(pl.multiple_of((1 - core) * 64, 64), 64), :], k_cov + g)
+    pltpu.make_async_copy(cmat.at[:, 0:64], cmat.at[:, 0:64], lsem.at[0]).wait()
+    arrived(cmat.at[:, 0:64], k_cov)
 
     mark("s31_product")
     pacc[...] = jnp.zeros((2, 64, 512), F32)
@@ -559,29 +572,31 @@
         return carry
 
     lax.fori_loop(0, 8, product, 0)
-    kp = take()
+    kp = take(precv)
     send(pacc.at[1 - core], precv, other, kp)
 
     mark("s32_f2wait")
-    for i in range(1, 8):
-        g = wrap(lat // 2 - i, 8)
-        arrived(fr.at[g // 2, lax.rem(g, 2)], kg + i - 1)
+    arrived(fr.at[:, :, 0:7], kg)
 
     mark("s33_freshprod")
 
     def fresh_product(g, acc):
-        f = fr[g // 2, lax.rem(g, 2)].reshape(16, 8, 128)
-        lanes = lax.broadcasted_iota(jnp.int32, (16, 8, 128), 2) // 8
+        f = fr[g // 2, lax.rem(g, 2)].reshape(16, 4, 128)
+        f = jnp.concatenate([f, f], axis=1)
+        lanes = (
+            lax.broadcasted_iota(jnp.int32, (16, 8, 128), 2) // 8
+            - lax.broadcasted_iota(jnp.int32, (16, 8, 128), 1) // 4 * 8
+        )
         w = jnp.concatenate([jnp.where(lanes == v, f, 0.0) for v in range(8)], axis=1)
         return acc + dot(cmat[g], w.astype(BF16).reshape(1024, 128))
 
-    added = lax.fori_loop(0, 8, fresh_product, jnp.zeros((128, 128), F32))
+    added = lax.fori_loop(0, 8, fresh_product, jnp.zeros((128, 128), F32), unroll=2)
     for shift in (64, 32, 16, 8):
         added = added + pltpu.roll(added, shift, 1)
     aacc[0] = added[0:64]
     aacc[1] = added[64:128]
     mark("s34_exch")
-    ka = take()
+    ka = take(arecv)
     send(aacc.at[1 - core], arecv, other, ka)
     arrived(precv, kp)
     arrived(arecv, ka)
@@ -594,14 +609,14 @@
             week_of == jnp.broadcast_to(week[...], (64, 128)), mine, 0.0
         )
     out_pre = load(pre, pre_h, 19)
-    for c in sends:
-        c.wait_send()
+    for view, k in sends:
+        remote(view, view, (lat, lon), k).wait_send()
     out_field.wait()
     out_pre.wait()
     mark("")
 
 
-COPIES = 240
+COPIES = 64
 UNROLL = 4
 PROFILE = False
 
@@ -622,8 +637,8 @@
             pltpu.VMEM((32, 128), F32),
             pltpu.VMEM((32, 128), jnp.int32),
             pltpu.VMEM((256, 128), jnp.int32),
-            pltpu.VMEM((1, 128), jnp.int32),
-            pltpu.VMEM((1, 128), jnp.int32),
+            pltpu.VMEM((1, 32), jnp.int32),
+            pltpu.VMEM((1, 1), jnp.int32),
             pltpu.VMEM((64, 416), BF16),
             pltpu.VMEM((8, 8, 32, 128), F32),
             pltpu.VMEM((8, 32, 128), F32),
@@ -631,7 +646,7 @@
             pltpu.VMEM((4, 2, 8, 2, 64, 128), BF16),
             pltpu.VMEM((4, 2, 8, 2, 64, 128), BF16),
             pltpu.VMEM((8, 128, 1024), BF16),
-            pltpu.VMEM((4, 2, 8, 2, 8, 128), F32),
+            pltpu.VMEM((4, 2, 8, 2, 4, 128), F32),
             pltpu.VMEM((4, 32, 128), F32),
             pltpu.VMEM((2, 64, 128), F32),
             pltpu.VMEM((2, 64, 128), F32),
@@ -653,7 +668,7 @@
             pltpu.VMEM((64, 512), F32),
             pltpu.SemaphoreType.DMA((COPIES,)),
             pltpu.SemaphoreType.DMA((COPIES,)),
-            pltpu.SemaphoreType.DMA((8,)),
+            pltpu.SemaphoreType.DMA((1,)),
             pltpu.SemaphoreType.DMA((20,)),
         ],
         compiler_params=pltpu.CompilerParams(
@@ -662,8 +677,7 @@
         name="window",
     )(
         adjoint, transport, cell_weight, region_local, tile_regions,
-        jnp.pad(polar_rows, (0, 96)).reshape(1, 128),
-        jnp.broadcast_to(week_index.reshape(1, 1), (1, 128)), grad_in, covariance,
+        polar_rows.reshape(1, 32), week_index.reshape(1, 1), grad_in, covariance,
     )
     return aout, pre[:, :416]
 

time: 79.2 us -> 67.6 us (0.85)
  Pallas kernels: 73.1 us -> 63.3 us
  local copies, waits for them, and re-layouts: 4.64 us -> 2.96 us
    pallas_call x1, Pallas kernels: 73.1 us -> 63.3 us  [shards(): pl.pallas_call(kernel, out_shape=(jax.ShapeDtypeStruct((8, 8, 32, 128), F...]
    reshape x1 -> x0, local copies, waits for them, and re-layouts: 1.17 us -> none  [shards(): jnp.pad(polar_rows, (0, 96)).reshape(1, 128)]
where the time goes in v3:
time: 67.6 us; the launch traced here: 67.5 us
  Pallas kernels  63.3 us (94%)
  local copies, waits for them, and re-layouts  2.96 us (4%)
  between operations  1.3 us (2%)
    pallas_call x1, Pallas kernels, shards(): pl.pallas_call(kernel, out_shape=(jax.ShapeDtypeStruct((8, 8, 32, 128), F...  63.3 us
    unnamed x4, local copies, waits for them, and re-layouts  2.96 us

profile of v3, /device:TPU:1, one launch (start us, length us, event | category | flops | bytes accessed | tf_op | source)
XLA Modules:
  0.0 67.5 jit_solution(1219206102024116998)
XLA Ops:
  1.3 63.3 %window.1 = (f32[8,8,32,128]{3,2,1,0:T(8,128)}, f32[64,512]{1,0:T(8,128)}) custom-call(f32[8,8,32,128]{3,2,1,0:T(8,128)} %adj_h.1, f32[6,8,32,128]{3,2,1,0:T(8,128)} %tr_h.1, f32[32,128]{1,0:T(8,128)} %weight_h.1, s32[32,128]{1,0:T(8,128)} %rl_h.1, s32[256,256]{1,0:T(8,128)} %tiles_h.1, s32[1,32]{1,0:T(1,128)} %bitcast.5, s32[1,1]{1,0:T(1,128)} %bitcast.3.week_h, ...), custom_call_target="tpu_custom_call" | custom-call | tf_op jit(solution)/shard_map/window/pallas_call | solution.py:626
  64.6 0.0 copy-start
  64.6 2.3 %copy.14 = f32[8,8,32,128]{3,2,1,0:T(8,128)} copy(f32[8,8,32,128]{3,2,1,0:T(8,128)} %get-tuple-element.8) | data formatting | bytes 2097152
  66.9 0.0 copy-done
  66.9 0.7 copy.15
Async XLA Ops:
  64.6 2.3 %copy-start = (f32[64,512]{1,0:T(8,128)S(1)}, f32[64,512]{1,0:T(8,128)}, u32[]{:S(2)}) copy-start(f32[64,512]{1,0:T(8,128)} %get-tuple-element.5) | copy-start | bytes 393220

commit v4 on v3

--- a/solution.py
+++ b/solution.py
@@ -244,9 +244,13 @@
         (((3, 1, 2),), ((3, 2, 2),)),
         (((3, 2, 0), (3, 2, 1), (3, 2, 2)), ()),
     )
-    long = short[:3] + (
-        short[3],
-        short[4],
+    long = (
+        ((), ((2, 1, 0),)),
+        (((2, 1, 0),), ((2, 2, 0),)),
+        ((), ((3, 1, 0), (3, 1, 1))),
+        (((2, 2, 0),), ((3, 1, 2),)),
+        (((3, 1, 0),), ((3, 2, 0),)),
+        (((3, 1, 1),), ((3, 2, 1),)),
         (((3, 2, 0),), ((3, 3, 0),)),
         (((3, 1, 2),), ((3, 2, 2),)),
         (((3, 2, 1),), ((3, 3, 1),)),
@@ -351,7 +355,6 @@
     col_s[3] = lax.fori_loop(16, 64, step_one(sides1b), rest1, unroll=UNROLL)
     k2b = halo_send(1, 1, 8, 64)
     mark("s09_pump")
-    pump("a", 1)
     pump("b", 2)
     pump("c", 2)
     mark("s10_halo2a")
@@ -377,10 +380,10 @@
         send(ybar.at[lon], ybar.at[lon], (lat, wrap(lon + i, 16)), kz)
     mark("s12_pump")
     pump("b", 3)
+    pump("a", 1)
     pump("c", 3)
+    pump("b", 4)
     mark("s15_pump")
-    pump("b", 4)
-    pump("c", 4)
     for c in in_late:
         c.wait()
     flags = 0.5 * jnp.sum(
@@ -418,9 +421,7 @@
         surf[t] = filtered(t, mean0) * weight[...]
 
     mark("s18_pump")
-    pump("a", 2)
-    pump("b", 5)
-    pump("c", 5)
+    pump("c", 4)
     mark("s19_regions")
 
     sub8 = lax.broadcasted_iota(jnp.int32, (16, 128), 0)
@@ -445,7 +446,7 @@
             acc = acc + dot_nt(left, jnp.concatenate(rhs[n], axis=1))
         return acc
 
-    m = lax.fori_loop(0, 16, regions, jnp.zeros((16, 128), F32), unroll=2)
+    m = lax.fori_loop(0, 16, regions, jnp.zeros((16, 128), F32), unroll=4)
     for i in range(16):
         mbuf[i] = m[i:i + 1, :]
     xbuf[lon] = mbuf[lon]
@@ -455,6 +456,10 @@
         send(mbuf.at[to], xbuf.at[lon], (lat, to), kx)
 
     mark("s13_halo2b")
+    pump("a", 2)
+    pump("b", 5)
+    pump("c", 5)
+    pump("b", 6)
     sides2b = halo_wait(1, 1, 8, 64, k2b)
     mark("s14_step2b")
     sums = lax.fori_loop(8, 64, step_two(sides2b), none, unroll=UNROLL)
@@ -465,7 +470,6 @@
     for i in range(1, 16):
         send(zbuf.at[lon], zbuf.at[lon], (lat, wrap(lon + i, 16)), kw)
     mark("s20_pump")
-    pump("b", 6)
     pump("c", 6)
     pump("a", 3)
     pump("b", 7)
@@ -510,6 +514,7 @@
     pump("a", 5)
     pump("c", 9)
     pump("b", 10)
+    pump("b", 11)
     arrived(obuf.at[0:15], ky)
 
     mark("s27_fresh")
@@ -522,7 +527,7 @@
             f = f + pltpu.roll(f, shift, 1)
         packed = jnp.where(lane8 // 8 == v, f, packed)
     packed = packed.astype(BF16).astype(F32)
-    fr[y, xl, z, xh] = packed[0:4] + pltpu.roll(packed[4:8], 64, 1)
+    fr[y, xl, z, xh] = (packed[0:4] + pltpu.roll(packed[4:8], 64, 1)).astype(BF16)
     kf = take(fr.at[0:3, 0, 0:5, 0])
     for i in range(1, 16):
         here = fr.at[y, xl, z, xh]
@@ -530,8 +535,8 @@
     mark("s28_pump")
     pump("a", 6)
     pump("c", 10)
-    pump("b", 11)
     pump("b", 12)
+    pump("b", 13)
     mark("s29_fwait")
     arrived(fr.at[0:3, 0, 0:5, 0], kf)
     kg = take(fr.at[:, :, 0:7])
@@ -541,7 +546,7 @@
     mark("s30_pump")
     pump("a", 7)
     pump("c", 11)
-    pump("b", 13)
+    pump("b", 14)
     pltpu.make_async_copy(cmat.at[:, 0:64], cmat.at[:, 0:64], lsem.at[0]).wait()
     arrived(cmat.at[:, 0:64], k_cov)
 
@@ -571,7 +576,7 @@
         pacc[1, :, 256:512] += right[64:128]
         return carry
 
-    lax.fori_loop(0, 8, product, 0)
+    lax.fori_loop(0, 8, product, 0, unroll=2)
     kp = take(precv)
     send(pacc.at[1 - core], precv, other, kp)
 
@@ -581,7 +586,7 @@
     mark("s33_freshprod")
 
     def fresh_product(g, acc):
-        f = fr[g // 2, lax.rem(g, 2)].reshape(16, 4, 128)
+        f = fr[g // 2, lax.rem(g, 2)].reshape(16, 4, 128).astype(F32)
         f = jnp.concatenate([f, f], axis=1)
         lanes = (
             lax.broadcasted_iota(jnp.int32, (16, 8, 128), 2) // 8
@@ -614,6 +619,25 @@
     out_field.wait()
     out_pre.wait()
     mark("")
+
+
+def finish(field, wide, aout, pre, held, block, trimmed, sem):
+    reads = [pltpu.make_async_copy(field.at[t], held.at[t], sem.at[t]) for t in range(8)]
+    small = pltpu.make_async_copy(wide, block, sem.at[8])
+    small.start()
+    for c in reads:
+        c.start()
+    small.wait()
+    trimmed[...] = block[:, 0:416]
+    writes = [pltpu.make_async_copy(trimmed, pre, sem.at[9])]
+    writes[0].start()
+    for t in range(8):
+        reads[t].wait()
+        c = pltpu.make_async_copy(held.at[t], aout.at[t], sem.at[10 + t])
+        c.start()
+        writes.append(c)
+    for c in writes:
+        c.wait()
 
 
 COPIES = 64
@@ -646,7 +670,7 @@
             pltpu.VMEM((4, 2, 8, 2, 64, 128), BF16),
             pltpu.VMEM((4, 2, 8, 2, 64, 128), BF16),
             pltpu.VMEM((8, 128, 1024), BF16),
-            pltpu.VMEM((4, 2, 8, 2, 4, 128), F32),
+            pltpu.VMEM((4, 2, 8, 2, 4, 128), BF16),
             pltpu.VMEM((4, 32, 128), F32),
             pltpu.VMEM((2, 64, 128), F32),
             pltpu.VMEM((2, 64, 128), F32),
@@ -679,7 +703,23 @@
         adjoint, transport, cell_weight, region_local, tile_regions,
         polar_rows.reshape(1, 32), week_index.reshape(1, 1), grad_in, covariance,
     )
-    return aout, pre[:, :416]
+    return pl.pallas_call(
+        finish,
+        out_shape=(
+            jax.ShapeDtypeStruct((8, 8, 32, 128), F32),
+            jax.ShapeDtypeStruct((64, 416), F32),
+        ),
+        in_specs=[hbm] * 2,
+        out_specs=(hbm, hbm),
+        scratch_shapes=[
+            pltpu.VMEM((8, 8, 32, 128), F32),
+            pltpu.VMEM((64, 512), F32),
+            pltpu.VMEM((64, 416), F32),
+            pltpu.SemaphoreType.DMA((18,)),
+        ],
+        compiler_params=pltpu.CompilerParams(vmem_limit_bytes=67043328),
+        name="finish",
+    )(aout, pre)
 
 
 def solution(mesh):

time: 67.6 us -> 64.6 us (0.956)
  local copies, waits for them, and re-layouts: 2.96 us -> 0 us
    unnamed x4 -> x0, local copies, waits for them, and re-layouts: 2.96 us -> none
    pallas_call x1, Pallas kernels: 63.3 us -> 61.1 us  [shards(): pl.pallas_call(kernel, out_shape=(jax.ShapeDtypeStruct((8, 8, 32, 128), F...]
    pallas_call x0 -> x1, Pallas kernels: none -> 2.15 us  [shards(): pl.pallas_call(finish, out_shape=(jax.ShapeDtypeStruct((8, 8, 32, 128), F...]
where the time goes in v4:
time: 64.6 us; the launch traced here: 64.5 us
  Pallas kernels  63.2 us (98%)
  between operations  1.29 us (2%)
    pallas_call x1, Pallas kernels, shards(): pl.pallas_call(kernel, out_shape=(jax.ShapeDtypeStruct((8, 8, 32, 128), F...  61.1 us
    pallas_call x1, Pallas kernels, shards(): pl.pallas_call(finish, out_shape=(jax.ShapeDtypeStruct((8, 8, 32, 128), F...  2.15 us

profile of v4, /device:TPU:1, one launch (start us, length us, event | category | flops | bytes accessed | tf_op | source)
XLA Modules:
  0.0 64.5 jit_solution(16652832865244365868)
XLA Ops:
  1.3 61.1 %window.1 = (f32[8,8,32,128]{3,2,1,0:T(8,128)}, f32[64,512]{1,0:T(8,128)}) custom-call(f32[8,8,32,128]{3,2,1,0:T(8,128)} %adj_h.1, f32[6,8,32,128]{3,2,1,0:T(8,128)} %tr_h.1, f32[32,128]{1,0:T(8,128)} %weight_h.1, s32[32,128]{1,0:T(8,128)} %rl_h.1, s32[256,256]{1,0:T(8,128)} %tiles_h.1, s32[1,32]{1,0:T(1,128)} %bitcast.3, s32[1,1]{1,0:T(1,128)} %bitcast.2.week_h, ...), custom_call_target="tpu_custom_call" | custom-call | tf_op jit(solution)/shard_map/window/pallas_call | solution.py:650
  62.3 2.1 %finish.1 = (f32[8,8,32,128]{3,2,1,0:T(8,128)}, f32[64,416]{1,0:T(8,128)}) custom-call(f32[8,8,32,128]{3,2,1,0:T(8,128)} %get-tuple-element.4.field, f32[64,512]{1,0:T(8,128)} %get-tuple-element.5.wide), custom_call_target="tpu_custom_call" | custom-call | tf_op jit(solution)/shard_map/finish/pallas_call | solution.py:706

commit v5 on v4

--- a/solution.py
+++ b/solution.py
@@ -355,8 +355,6 @@
     col_s[3] = lax.fori_loop(16, 64, step_one(sides1b), rest1, unroll=UNROLL)
     k2b = halo_send(1, 1, 8, 64)
     mark("s09_pump")
-    pump("b", 2)
-    pump("c", 2)
     mark("s10_halo2a")
     sides2a = halo_wait(1, 0, 0, 8, k2a)
     mark("s11_step2a")
@@ -379,6 +377,8 @@
     for i in range(1, 16):
         send(ybar.at[lon], ybar.at[lon], (lat, wrap(lon + i, 16)), kz)
     mark("s12_pump")
+    pump("b", 2)
+    pump("c", 2)
     pump("b", 3)
     pump("a", 1)
     pump("c", 3)
@@ -576,7 +576,7 @@
         pacc[1, :, 256:512] += right[64:128]
         return carry
 
-    lax.fori_loop(0, 8, product, 0, unroll=2)
+    lax.fori_loop(0, 8, product, 0, unroll=4)
     kp = take(precv)
     send(pacc.at[1 - core], precv, other, kp)
 
@@ -595,7 +595,7 @@
         w = jnp.concatenate([jnp.where(lanes == v, f, 0.0) for v in range(8)], axis=1)
         return acc + dot(cmat[g], w.astype(BF16).reshape(1024, 128))
 
-    added = lax.fori_loop(0, 8, fresh_product, jnp.zeros((128, 128), F32), unroll=2)
+    added = lax.fori_loop(0, 8, fresh_product, jnp.zeros((128, 128), F32), unroll=4)
     for shift in (64, 32, 16, 8):
         added = added + pltpu.roll(added, shift, 1)
     aacc[0] = added[0:64]

time: 64.6 us -> 65.3 us (1.011)
  Pallas kernels: 63.2 us -> 63.9 us
    pallas_call x1, Pallas kernels: 61.1 us -> 61.7 us  [shards(): pl.pallas_call(kernel, out_shape=(jax.ShapeDtypeStruct((8, 8, 32, 128), F...]
where the time goes in v5:
time: 65.3 us; the launch traced here: 65.2 us
  Pallas kernels  63.9 us (98%)
  between operations  1.29 us (2%)
    pallas_call x1, Pallas kernels, shards(): pl.pallas_call(kernel, out_shape=(jax.ShapeDtypeStruct((8, 8, 32, 128), F...  61.7 us
    pallas_call x1, Pallas kernels, shards(): pl.pallas_call(finish, out_shape=(jax.ShapeDtypeStruct((8, 8, 32, 128), F...  2.15 us

profile of v5, /device:TPU:1, one launch (start us, length us, event | category | flops | bytes accessed | tf_op | source)
XLA Modules:
  0.0 65.2 jit_solution(6146217197995521641)
XLA Ops:
  1.3 61.7 %window.1 = (f32[8,8,32,128]{3,2,1,0:T(8,128)}, f32[64,512]{1,0:T(8,128)}) custom-call(f32[8,8,32,128]{3,2,1,0:T(8,128)} %adj_h.1, f32[6,8,32,128]{3,2,1,0:T(8,128)} %tr_h.1, f32[32,128]{1,0:T(8,128)} %weight_h.1, s32[32,128]{1,0:T(8,128)} %rl_h.1, s32[256,256]{1,0:T(8,128)} %tiles_h.1, s32[1,32]{1,0:T(1,128)} %bitcast.3, s32[1,1]{1,0:T(1,128)} %bitcast.2.week_h, ...), custom_call_target="tpu_custom_call" | custom-call | tf_op jit(solution)/shard_map/window/pallas_call | solution.py:650
  63.0 2.1 %finish.1 = (f32[8,8,32,128]{3,2,1,0:T(8,128)}, f32[64,416]{1,0:T(8,128)}) custom-call(f32[8,8,32,128]{3,2,1,0:T(8,128)} %get-tuple-element.4.field, f32[64,512]{1,0:T(8,128)} %get-tuple-element.5.wide), custom_call_target="tpu_custom_call" | custom-call | tf_op jit(solution)/shard_map/finish/pallas_call | solution.py:706

commit v6 on v4

--- a/solution.py
+++ b/solution.py
@@ -286,12 +286,10 @@
                 ring_start(p, *w)
 
     k1a = halo_send(0, 0, 0, 16)
-    for c in in_adj[2:]:
-        c.wait()
-    col_s[1] = lax.fori_loop(16, 64, pack, none, unroll=4)
-
     for c in in_grad:
         c.wait()
+    for p in "bc":
+        direct_start(p)
     tail = jnp.zeros((16, 128), F32)
     for q in range(4):
         sel = (
@@ -301,9 +299,12 @@
         tail = tail + dot(gtail[16 * q:16 * q + 16, 384:416], sel)
     b0[y, xl, z, xh, 64:80, :] = tail.astype(BF16)
 
+    direct_start("a")
+    for c in in_adj[2:]:
+        c.wait()
+    col_s[1] = lax.fori_loop(16, 64, pack, none, unroll=4)
+
     k1b = halo_send(0, 1, 16, 64)
-    for p in "bac":
-        direct_start(p)
     k_cov = take(cmat.at[:, 0:64])
     for g in range(8):
         send(
@@ -595,7 +596,7 @@
         w = jnp.concatenate([jnp.where(lanes == v, f, 0.0) for v in range(8)], axis=1)
         return acc + dot(cmat[g], w.astype(BF16).reshape(1024, 128))
 
-    added = lax.fori_loop(0, 8, fresh_product, jnp.zeros((128, 128), F32), unroll=2)
+    added = lax.fori_loop(0, 8, fresh_product, jnp.zeros((128, 128), F32), unroll=4)
     for shift in (64, 32, 16, 8):
         added = added + pltpu.roll(added, shift, 1)
     aacc[0] = added[0:64]

time: 64.6 us -> 64.7 us (level)
  no operation moved by 1% of the time
where the time goes in v6:
time: 64.7 us; the launch traced here: 64.6 us
  Pallas kernels  63.3 us (98%)
  between operations  1.29 us (2%)
    pallas_call x1, Pallas kernels, shards(): pl.pallas_call(kernel, out_shape=(jax.ShapeDtypeStruct((8, 8, 32, 128), F...  61.2 us
    pallas_call x1, Pallas kernels, shards(): pl.pallas_call(finish, out_shape=(jax.ShapeDtypeStruct((8, 8, 32, 128), F...  2.15 us

profile of v6, /device:TPU:1, one launch (start us, length us, event | category | flops | bytes accessed | tf_op | source)
XLA Modules:
  0.0 64.6 jit_solution(18200613142773314174)
XLA Ops:
  1.3 61.2 %window.1 = (f32[8,8,32,128]{3,2,1,0:T(8,128)}, f32[64,512]{1,0:T(8,128)}) custom-call(f32[8,8,32,128]{3,2,1,0:T(8,128)} %adj_h.1, f32[6,8,32,128]{3,2,1,0:T(8,128)} %tr_h.1, f32[32,128]{1,0:T(8,128)} %weight_h.1, s32[32,128]{1,0:T(8,128)} %rl_h.1, s32[256,256]{1,0:T(8,128)} %tiles_h.1, s32[1,32]{1,0:T(1,128)} %bitcast.3, s32[1,1]{1,0:T(1,128)} %bitcast.2.week_h, ...), custom_call_target="tpu_custom_call" | custom-call | tf_op jit(solution)/shard_map/window/pallas_call | solution.py:651
  62.5 2.1 %finish.1 = (f32[8,8,32,128]{3,2,1,0:T(8,128)}, f32[64,416]{1,0:T(8,128)}) custom-call(f32[8,8,32,128]{3,2,1,0:T(8,128)} %get-tuple-element.4.field, f32[64,512]{1,0:T(8,128)} %get-tuple-element.5.wide), custom_call_target="tpu_custom_call" | custom-call | tf_op jit(solution)/shard_map/finish/pallas_call | solution.py:707
